TPU v7x, 128 devices: a whole 4x4x4 slice. The times are simulated.
128 devices in a mesh: row: 16 (over z, x), col: 8 (over y, core).
Axes of the slice: x: 4, y: 4, z: 4, core: 2. Of those that a mesh axis runs over, the one named last changes fastest.
Arguments:
- pole_values: float32 [65536], P('row'), may hold values from -32768 to 32768, as said below
- weights: float32 [65536], P('row'), may hold values from 0.15 to 0.5
- centers: float32 [65536], P('col'), as said below
- offsets: float32 [65536], P('col'), may hold values from -0.1 to 0.1
- chosen: int32 [2048], replicated, may hold values from 0 to 65535
- column_pole: int32 [2, 32768], P(None, 'row'), may hold values from 0 to 65535, as said below
- eigen_blocks: bfloat16 [6144, 2, 32768], P('col', None, 'row'), may hold values from -6 to 6
Outputs:
- roots_offset: float32 [65536], P('col')
- panel: float32 [6144, 2, 2048], P(('col', 'row'))
Inputs may be any that keep to these rules, and one draw needn't show every extreme that they name: `pole_values`: ascending; consecutive poles differ by 1/4 to 7/4; every pole is a multiple of 1/128. centers[i] is the midpoint of pole_values[i] and pole_values[i + 1]; the last one is the last pole plus 1/2. `chosen`: indices of roots. `column_pole`: each of 0 to 65535 stands once.
All inputs are finite; a program needn't handle non-finite values.
Results may differ from a plain program's by a relative error of at most 0.0021.
Values may be sent and summed in bfloat16 or wider, within the bound.
A program may use at most 128 MiB of HBM per device.

v0:
```python
import jax
import jax.numpy as jnp
from jax import lax
from jax.sharding import Mesh
from jax.sharding import PartitionSpec as P

ITERS = 3
ROW = ("row_0", "row_1")
COL_ROW = ("col", "row_0", "row_1")


def gather_turned(arrays, axis, dims):
    turned = [jnp.moveaxis(a, dim, 0) for a, dim in zip(arrays, dims)]
    widths = [t[0].size for t in turned]
    both = jnp.concatenate([t.reshape(-1, w) for t, w in zip(turned, widths)], axis=1)
    filled = lax.all_gather(both, axis, axis=0, tiled=True)
    blocks = jnp.split(filled, [sum(widths[:k]) for k in range(1, len(widths))], axis=1)
    return tuple(
        (
            jnp.moveaxis(b.reshape(-1, *t.shape[1:]), 0, dim)
            for b, t, dim in zip(blocks, turned, dims)
        )
    )


def copy_for_each(shard, axis):
    size = lax.axis_size(axis)
    return lax.all_to_all(
        jnp.broadcast_to(shard[None], (size, *shard.shape)), axis, 0, 0, tiled=True
    )


def joined_along(blocks, dim):
    blocks = jnp.moveaxis(blocks, 0, dim)
    lengths = blocks.shape
    return blocks.reshape(*lengths[:dim], lengths[dim] * lengths[dim + 1], *lengths[dim + 2 :])


def gather_directly(shard, axis, dim):
    blocks = copy_for_each(shard, axis)
    return joined_along(blocks, dim)


def by_axis(shard, axes):
    for axis in axes:
        shard = lax.psum(shard, axis)
    return shard


def block_sums(pole_vals, weight_sq, center_vals, offset_vals, block_rows):
    root_count = center_vals.shape[0]
    block_rows = min(block_rows, root_count)
    center_blocks = center_vals.reshape(root_count // block_rows, block_rows)
    offset_blocks = offset_vals.reshape(root_count // block_rows, block_rows)

    def per_block(blocks):
        distance = pole_vals[None, :] - blocks[0][:, None] - blocks[1][:, None]
        inverse = 1.0 / distance
        weighted = weight_sq[None, :] * inverse
        return (
            jnp.sum(weighted, axis=1),
            jnp.sum(weighted * inverse, axis=1),
            jnp.min(jnp.abs(distance), axis=1),
        )

    sums = lax.map(per_block, (center_blocks, offset_blocks))
    return tuple((item.reshape(root_count) for item in sums))


def newton_update(offset_now, sum_inverse, sum_square, nearest):
    limit = 0.5 * nearest
    return offset_now - jnp.clip((1.0 + sum_inverse) / sum_square, -limit, limit)


def cauchy_block(pole_picked, weight_picked, panel_center, panel_offset, inv_norm):
    distance = pole_picked[:, None] - panel_center[None, :] - panel_offset[None, :]
    return (weight_picked[:, None] * (1.0 / distance) * inv_norm[None, :]).astype(jnp.bfloat16)


def on_device(pole_values, weights, centers, offsets, chosen, column_pole, eigen_blocks):
    all_poles, all_weights = gather_turned((pole_values, weights), ROW, (0, 0))
    weight_sq = weights * weights
    per_device = offsets.shape[0] // lax.axis_size(ROW)
    first_root = lax.axis_index(ROW) * per_device
    my_centers = lax.dynamic_slice_in_dim(centers, first_root, per_device)
    my_offsets = lax.dynamic_slice_in_dim(offsets, first_root, per_device)
    all_sq = all_weights * all_weights
    for iteration in range(ITERS):
        sum_inverse, sum_square, nearest = block_sums(all_poles, all_sq, my_centers, my_offsets, 32)
        my_offsets = newton_update(my_offsets, sum_inverse, sum_square, nearest)
    offset_now = gather_directly(my_offsets, ROW, 0)
    full_centers, full_offsets = gather_turned((centers, offset_now), "col", (0, 0))
    panel_center = full_centers[chosen]
    panel_offset = full_offsets[chosen]
    partial_sq = block_sums(pole_values, weight_sq, panel_center, panel_offset, 64)[1]
    norm_sq = by_axis(partial_sq, ROW)
    inv_norm = lax.rsqrt(norm_sq)
    cauchy_halves = []
    for half_index in range(2):
        pole_index = column_pole[half_index]
        cauchy_halves.append(
            cauchy_block(
                all_poles[pole_index], all_weights[pole_index], panel_center, panel_offset, inv_norm
            )
        )
    panel = lax.psum_scatter(
        jnp.stack(
            [
                jnp.dot(
                    eigen_blocks[:, half_index, :],
                    cauchy_halves[half_index],
                    preferred_element_type=jnp.float32,
                )
                for half_index in range(2)
            ],
            axis=1,
        ),
        ROW,
        scatter_dimension=0,
        tiled=True,
    )
    return (offset_now, panel)


def solution(mesh):
    torus = Mesh(mesh.devices.reshape(4, 4, mesh.shape["col"]), ("row_0", "row_1", "col"))
    placed = (P(ROW), P(ROW), P("col"), P("col"), P(), P(None, ROW), P("col", None, ROW))
    return jax.shard_map(
        on_device,
        mesh=torus,
        in_specs=placed,
        out_specs=(P("col"), P(COL_ROW, None, None)),
        check_vma=False,
    )
```

profile of v0, /device:TPU:8, one launch (start us, length us, event | category | flops | bytes accessed | tf_op | source)
XLA Modules:
  0.0 556.5 jit_solution(9556216317746386524)
XLA Ops:
  9.6 25.4 %all_gather.6 = f32[65536,2]{0,1:T(2,128)S(1)} all-gather(f32[4096,2]{0,1:T(2,128)S(1)} %pad_maximum_fusion.2), channel_id=1, replica_groups=mesh['row_0'=4,'row_1'=4,'col'=8] {'row_0','row_1'}, dimensions={0}, use_global_device_ids=true | all-gather | bytes 557056 | tf_op jit(solution)/shard_map/all_gather | solution.py:16
  35.5 46.1 %while.52 = (s32[]{:T(128)}, f32[16,32]{1,0:T(8,128)S(1)}, f32[16,32]{1,0:T(8,128)S(1)}, f32[16,32]{1,0:T(8,128)S(1)}, f32[65536]{0:T(1024)S(1)}, /*index=5*/f32...) while((s32[]{:T(128)}, f32[16,32]{1,0:T(8,128)S(1)}, ...), condition=%wide.region_4.5_spmd, body=%wide.region_0.4_spmd.sunk | while | flops 18874272 | bytes 526325 | solution.py:66
  52.8 2.7 fusion.33
  82.6 46.1 %while.53 = (s32[]{:T(128)}, f32[16,32]{1,0:T(8,128)S(1)}, f32[16,32]{1,0:T(8,128)S(1)}, f32[16,32]{1,0:T(8,128)S(1)}, f32[65536]{0:T(1024)S(1)}, /*index=5*/f32...) while((s32[]{:T(128)}, f32[16,32]{1,0:T(8,128)S(1)}, ...), condition=%wide.region_9.10_spmd, body=%wide.region_5.9_spmd.sunk | while | flops 18874272 | bytes 526325 | solution.py:66
  108.5 2.7 fusion.34
  128.9 46.1 %while.54 = (s32[]{:T(128)}, f32[16,32]{1,0:T(8,128)S(1)}, f32[16,32]{1,0:T(8,128)S(1)}, f32[16,32]{1,0:T(8,128)S(1)}, f32[65536]{0:T(1024)S(1)}, /*index=5*/f32...) while((s32[]{:T(128)}, f32[16,32]{1,0:T(8,128)S(1)}, ...), condition=%wide.region_14.15_spmd, body=%wide.region_10.14_spmd.sunk | while | flops 18874272 | bytes 526325 | solution.py:66
  134.7 2.7 fusion.35
  175.8 4.9 all-to-all-start
  180.9 13.8 %fusion.26 = (bf16[768,1,2048]{2,1,0:T(2,128)(2,1)}, bf16[768,1,2048]{2,1,0:T(2,128)(2,1)}) fusion(bf16[768,2,2048]{2,1,0:T(2,128)(2,1)} %param.21), kind=kLoop, calls=%fused_computation.75 | loop fusion | bytes 12582912 | tf_op jit(solution)/shard_map/slice | solution.py:110
  194.8 11.8 %gather_fusion = f32[2048]{0:T(1024)S(1)} fusion(f32[65536]{0:T(1024)S(1)} %bitcast.100, s32[2048]{0:T(1024)S(1)} %broadcast_clamp_fusion.1), kind=kCustom, calls=%fused_computation | custom fusion | bytes 24576 | tf_op jit(solution)/shard_map/gather | solution.py:103
  206.5 11.8 %gather_fusion.1 = f32[2048]{0:T(1024)S(1)} fusion(f32[65536]{0:T(1024)S(1)} %bitcast.96, s32[2048]{0:T(1024)S(1)} %broadcast_clamp_fusion.1), kind=kCustom, calls=%fused_computation.1 | custom fusion | bytes 24576 | tf_op jit(solution)/shard_map/gather | solution.py:103
  218.4 11.8 %gather_fusion.5 = f32[2048]{0:T(1024)S(1)} fusion(f32[65536]{0:T(1024)S(1)} %bitcast.97, s32[2048]{0:T(1024)S(1)} %broadcast_clamp_fusion), kind=kCustom, calls=%fused_computation.5 | custom fusion | bytes 24576 | tf_op jit(solution)/shard_map/gather | solution.py:103
  230.1 11.8 %gather_fusion.4 = f32[2048]{0:T(1024)S(1)} fusion(f32[65536]{0:T(1024)S(1)} %bitcast.101, s32[2048]{0:T(1024)S(1)} %broadcast_clamp_fusion), kind=kCustom, calls=%fused_computation.4 | custom fusion | bytes 24576 | tf_op jit(solution)/shard_map/gather | solution.py:103
  242.0 13.3 %all_gather.7 = f32[65536,2]{0,1:T(2,128)S(1)} all-gather(f32[8192,2]{0,1:T(2,128)S(1)} %pad_maximum_fusion.1), channel_id=1, replica_groups=mesh['row_0'=4,'row_1'=4,'col'=8] {'col'}, dimensions={0}, use_global_device_ids=true | all-gather | bytes 589824 | tf_op jit(solution)/shard_map/all_gather | solution.py:16
  255.8 11.8 %gather_fusion.2 = f32[2048]{0:T(1024)S(1)} fusion(f32[65536]{0:T(1024)S(1)} %bitcast.103, s32[2048]{0:T(1024)S(1)} %fusion.23), kind=kCustom, calls=%fused_computation.2 | custom fusion | bytes 24576 | tf_op jit(solution)/shard_map/gather | solution.py:93
  267.6 11.8 %gather_fusion.3 = f32[2048]{0:T(1024)S(1)} fusion(f32[65536]{0:T(1024)S(1)} %bitcast.102, s32[2048]{0:T(1024)S(1)} %fusion.23), kind=kCustom, calls=%fused_computation.3 | custom fusion | bytes 24576 | tf_op jit(solution)/shard_map/gather | solution.py:94
  279.5 14.2 %while.55 = (s32[]{:T(128)}, f32[32,64]{1,0:T(8,128)S(1)}, f32[4096]{0:T(1024)S(1)}, f32[4096]{0:T(1024)S(1)}, f32[32,64]{1,0:T(8,128)S(1)}, /*index=5*/f32[32,64]{1,0:T(8,128)S(1)}, s32[]{:T(128)}, s32[]{:T(128)}) while((s32[]{:T(128)}, f32[32,64]{1,0:T(8,128)S(1)}, f32[4096]{0:T(1024)S(1)}, f32[4096]{0:T(1024)S(1)}, ...), condition=%wide.region_17.18_spmd, body=%wide.region_15.17_spmd.sunk | while | flops 1572802 | bytes 35165 | solution.py:66
  293.8 10.9 %psum.14 = f32[2048]{0:T(1024)S(1)} all-reduce(f32[2048]{0:T(1024)S(1)} %reshape.184), channel_id=1, replica_groups=mesh['row_0'=4,'row_1'=4,'col'=8] {'row_0'}, use_global_device_ids=true, to_apply=%region_18.19 | all-reduce | flops 2048 | bytes 16384 | tf_op jit(solution)/shard_map/psum | solution.py:46
  304.7 10.7 %psum.15 = f32[2048]{0:T(1024)S(1)} all-reduce(f32[2048]{0:T(1024)S(1)} %psum.14), channel_id=1, replica_groups=mesh['row_0'=4,'row_1'=4,'col'=8] {'row_1'}, use_global_device_ids=true, to_apply=%region_19.20 | all-reduce | flops 2048 | bytes 16384 | tf_op jit(solution)/shard_map/psum | solution.py:46
  315.4 14.9 %fusion.22 = f32[768,1,2048]{0,2,1:T(8,128)} fusion(f32[2048]{0:T(1024)S(1)} %rsqrt.3, f32[2048]{0:T(1024)S(1)} %gather_fusion.3, f32[2048]{0:T(1024)S(1)} %gather_fusion.2, f32[2048]{0:T(1024)S(1)} %gather_fusion.1, f32[2048]{0:T(1024)S(1)} %gather_fusion, bf16[768,1,2048]{2,1,0:T(2,128)(2,1)} %get-tuple-element.257), kind=kOutput, calls=%fused_computation.52 | convolution fusion | flops 6467616768 | bytes 9478144 | tf_op jit(solution)/shard_map/dot_general | solution.py:109
  330.3 12.2 %fusion.21 = f32[768,1,2048]{0,2,1:T(8,128)} fusion(f32[2048]{0:T(1024)S(1)} %gather_fusion.5, f32[2048]{0:T(1024)S(1)} %gather_fusion.4, f32[2048]{0:T(1024)S(1)} %rsqrt.3, f32[2048]{0:T(1024)S(1)} %gather_fusion.3, f32[2048]{0:T(1024)S(1)} %gather_fusion.2, bf16[768,1,2048]{2,1,0:T(2,128)(2,1)S(1)} %bitcast.105), kind=kOutput, calls=%fused_computation.51 | convolution fusion | flops 6467616768 | bytes 9478144 | tf_op jit(solution)/shard_map/dot_general | solution.py:109
  342.5 10.0 %pad_maximum_fusion = f32[768,2,2048]{0,2,1:T(8,128)} fusion(f32[768,1,2048]{0,2,1:T(8,128)} %fusion.21, f32[768,1,2048]{0,2,1:T(8,128)} %fusion.22), kind=kLoop, calls=%fused_computation.36 | loop fusion | flops 3145728 | bytes 25165824 | tf_op jit(solution)/shard_map/stack | solution.py:107
  352.5 19.4 %copy.18 = f32[768,2,2048]{2,1,0:T(2,128)} copy(f32[768,2,2048]{0,2,1:T(8,128)} %pad_maximum_fusion) | data formatting | bytes 25165824 | tf_op jit(solution)/shard_map/stack | solution.py:107
  373.8 173.2 %all-reduce.3.cloned.1.call-done = f32[768,2,2048]{2,1,0:T(2,128)} async-done(((f32[768,2,2048]{2,1,0:T(2,128)}), f32[768,2,2048]{2,1,0:T(2,128)}) %all-reduce.3.cloned.1.call-update) | async-done | bytes 12582928
  (401 shorter events, 152.0 us)
Async XLA Ops:
  7.2 173.6 %copy-start.4 = (s32[2048]{0:T(1024)S(1)}, s32[2048]{0:T(1024)}, u32[]{:S(2)}) copy-start(s32[2048]{0:T(1024)} %param.19) | copy-start | bytes 24580
  7.2 173.7 %copy-start.3 = (s32[2,2048]{1,0:T(2,128)S(1)}, s32[2,2048]{1,0:T(2,128)}, u32[]{:S(2)}) copy-start(s32[2,2048]{1,0:T(2,128)} %param.20) | copy-start | bytes 49156
  175.8 66.1 %all-to-all-start = ((f32[16,1,512]{2,1,0:T(1,128)}), f32[16,1,512]{2,1,0:T(1,128)S(1)}, u32[]{:S(2)}, u32[]{:S(2)}) async-start(f32[16,1,512]{2,1,0:T(1,128)} %broadcast_in_dim.72), calls=%async_computation | async-start | bytes 65536 | tf_op jit(solution)/shard_map/all_to_all | solution.py:28
  180.8 366.3 %all-reduce.3.cloned.1.call-start = ((), (), s32[]{:S(2)}) async-start(), calls=%async_computation.1 | async-start | bytes 25165824
  180.9 13.9 %copy-start.1 = (f32[4096]{0:T(1024)S(1)}, f32[4096]{0:T(1024)}, u32[]{:S(2)}) copy-start(f32[4096]{0:T(1024)} %param.16) | copy-start | bytes 49156
  218.3 23.6 %copy-start.2 = (f32[8192]{0:T(1024)S(1)}, f32[8192]{0:T(1024)}, u32[]{:S(2)}) copy-start(f32[8192]{0:T(1024)} %param.17) | copy-start | bytes 98308
  255.8 23.7 %copy-start = (f32[4096]{0:T(1024)S(1)}, f32[4096]{0:T(1024)}, u32[]{:S(2)}) copy-start(f32[4096]{0:T(1024)} %param.15) | copy-start | bytes 49156
  267.6 62.7 %slice-start = ((s8[6291456]{0:T(1024)(128)(4,1)}), s8[2097152]{0:T(1024)(128)(4,1)S(1)}, s32[]{:S(2)}) async-start(s8[6291456]{0:T(1024)(128)(4,1)} %bitcast.104), calls=%async_computation.2 | async-start | bytes 4194304
  315.4 14.9 %slice-start.1 = ((s8[6291456]{0:T(1024)(128)(4,1)}), s8[4194304]{0:T(1024)(128)(4,1)S(1)}, s32[]{:S(2)}) async-start(s8[6291456]{0:T(1024)(128)(4,1)} %bitcast.104), calls=%async_computation.3 | async-start | bytes 8388608
  371.9 0.7 copy-start.5
Sparse Core Ops, SparseCore 0:
  372.0 174.9 all-reduce.2
where the time goes:
time: 558 us; the launch traced here: 557 us
  waiting for transfers between devices  173 us (31%)
  other arithmetic  155 us (28%)
  local copies, waits for them, and re-layouts  119 us (21%)
  blocking collectives  60.3 us (11%)
  matrix products  27 us (5%)
  between operations  15 us (3%)
    unnamed x2, waiting for transfers between devices  173 us
    reduce_sum x80, other arithmetic, per_block(): jnp.sum(weighted * inverse, axis=1)  143 us
    all_gather x2, blocking collectives, gather_turned(): filled = lax.all_gather(both, axis, axis=0, tiled=True)  38.7 us
    dot_general x2, matrix products, on_device(): jnp.dot(eigen_blocks[:, half_index, :], cauchy_halves[half_index], prefer...  27 us
    gather x2, local copies, waits for them, and re-layouts, on_device(): all_weights[pole_index]  23.6 us
    gather x2, local copies, waits for them, and re-layouts, on_device(): all_poles[pole_index]  23.6 us
    psum x2, blocking collectives, by_axis(): shard = lax.psum(shard, axis)  21.6 us
    another operation x1, local copies, waits for them, and re-layouts, on_device(): jnp.stack([jnp.dot(eigen_blocks[:, half_index, :], cauchy_halves[half_ind...  19.4 us
  transfers between devices with their start and end apart: 2, of which 1 were waited for; matrix products, arithmetic and copies ran while one was open for 11% of the time, Pallas kernels for 0%

commit v1 on v0

v1 whole, which is shorter than its diff:
```python
import functools

import jax
import jax.numpy as jnp
from jax import lax
from jax.experimental import pallas as pl
from jax.experimental.pallas import tpu as pltpu
from jax.sharding import PartitionSpec as P

MESH = pl.DeviceIdType.MESH
VMEM = pltpu.VMEM
F32 = jnp.float32
BF16 = jnp.bfloat16
ROWS, COLS = 16, 8
N = 65536
TILES = N // 128
PANEL = 2048
MINE = 16
ITERS = 3


def vmem():
    return pl.BlockSpec(memory_space=VMEM)


def greet(row, col):
    barrier = pltpu.get_barrier_semaphore()
    for j in range(1, ROWS):
        pl.semaphore_signal(barrier, inc=1, device_id={"row": lax.rem(row + j, ROWS)}, device_id_type=MESH)
    for j in range(1, COLS):
        pl.semaphore_signal(barrier, inc=1, device_id={"col": lax.rem(col + j, COLS)}, device_id_type=MESH)
    pl.semaphore_wait(barrier, ROWS + COLS - 2)


def spread(src, dst, axis, size, me, send, recv):
    out = []
    for j in range(1, size):
        copy = pltpu.make_async_remote_copy(
            src_ref=src,
            dst_ref=dst.at[me],
            send_sem=send.at[j - 1],
            recv_sem=recv.at[j - 1],
            device_id={axis: lax.rem(me + j, size)},
            device_id_type=MESH,
        )
        copy.start()
        out.append(copy)
    return out


def collect(copies, src, dst, axis, size, me, send, recv):
    for j, copy in enumerate(copies, 1):
        got = pltpu.make_async_remote_copy(
            src_ref=src,
            dst_ref=dst.at[lax.rem(me + size - j, size)],
            send_sem=send.at[j - 1],
            recv_sem=recv.at[j - 1],
            device_id={axis: lax.rem(me + j, size)},
            device_id_type=MESH,
        )
        got.wait_recv()
        copy.wait_send()


def gather_kernel(p_ref, w_ref, o_ref, p_out, w_out, o_out, ps, pr, ws, wr, os_, or_, ls):
    row, col = lax.axis_index("row"), lax.axis_index("col")
    own = [
        pltpu.make_async_copy(p_ref, p_out.at[row], ls.at[0]),
        pltpu.make_async_copy(w_ref, w_out.at[row], ls.at[1]),
        pltpu.make_async_copy(o_ref, o_out.at[col], ls.at[2]),
    ]
    for c in own:
        c.start()
    greet(row, col)
    a = spread(p_ref, p_out, "row", ROWS, row, ps, pr)
    b = spread(w_ref, w_out, "row", ROWS, row, ws, wr)
    c = spread(o_ref, o_out, "col", COLS, col, os_, or_)
    collect(a, p_ref, p_out, "row", ROWS, row, ps, pr)
    collect(b, w_ref, w_out, "row", ROWS, row, ws, wr)
    collect(c, o_ref, o_out, "col", COLS, col, os_, or_)
    for c in own:
        c.wait()


def dma(n):
    return pltpu.SemaphoreType.DMA((n,))


def gather_all(poles, weights, offsets):
    return pl.pallas_call(
        gather_kernel,
        name="gather_all",
        out_shape=(
            jax.ShapeDtypeStruct((ROWS, 32, 128), F32),
            jax.ShapeDtypeStruct((ROWS, 32, 128), F32),
            jax.ShapeDtypeStruct((COLS, 64, 128), F32),
        ),
        in_specs=[vmem()] * 3,
        out_specs=(vmem(),) * 3,
        scratch_shapes=[dma(15), dma(15), dma(15), dma(15), dma(7), dma(7), dma(3)],
        compiler_params=pltpu.CompilerParams(collective_id=0, has_side_effects=True),
    )(poles.reshape(32, 128), weights.reshape(32, 128), offsets.reshape(64, 128))


def limited(t, s1, s2, nearest):
    limit = 0.5 * nearest
    return t - jnp.clip((1.0 + s1) / s2, -limit, limit)


def pieces(x):
    hi = x.astype(BF16)
    rest = x - hi.astype(F32)
    mid = rest.astype(BF16)
    low = (rest - mid.astype(F32)).astype(BF16)
    return hi, mid, low


def panel_roots_kernel(ch_ref, p_ref, w_ref, off_ref, cp_ref, tbl_ref, pw_ref, w2, sp, sq, st, sl):
    row, col = lax.axis_index("row"), lax.axis_index("col")
    dev = row * COLS + col
    lane = lax.broadcasted_iota(jnp.int32, (1, 128), 1)
    w2[...] = w_ref[...] * w_ref[...]
    for i in range(MINE):
        r = ch_ref[i * 128 + dev]
        r1 = jnp.minimum(r + 1, N - 1)
        sp[i : i + 1, :] = jnp.where(lane == (r & 127), p_ref[pl.ds(r >> 7, 1), :], 0.0)
        sq[i : i + 1, :] = jnp.where(lane == (r1 & 127), p_ref[pl.ds(r1 >> 7, 1), :], 0.0)
        st[i : i + 1, :] = jnp.where(lane == (r & 127), off_ref[pl.ds(r >> 7, 1), :], 0.0)
        sl[i : i + 1, :] = jnp.broadcast_to(jnp.where(r == N - 1, 1.0, 0.0), (1, 128))

    def wide(ref):
        return jnp.broadcast_to(jnp.sum(ref[...], axis=1, keepdims=True), (MINE, 128))

    p0, p1, t = wide(sp), wide(sq), wide(st)
    last = sl[...] > 0.5
    c = jnp.where(last, p0 + 0.5, 0.5 * (p0 + p1))
    h = c - p0

    def sums(t):
        def step(s, carry):
            s1, s2 = carry
            for k in range(8):
                pole = p_ref[pl.ds(s * 8 + k, 1), :]
                wsq = w2[pl.ds(s * 8 + k, 1), :]
                inverse = 1.0 / ((pole - c) - t)
                weighted = wsq * inverse
                s1 = s1 + weighted
                s2 = s2 + weighted * inverse
            return s1, s2

        zero = jnp.zeros((MINE, 128), F32)
        s1, s2 = lax.fori_loop(0, TILES // 8, step, (zero, zero))
        return (
            jnp.broadcast_to(jnp.sum(s1, axis=1, keepdims=True), (MINE, 128)),
            jnp.broadcast_to(jnp.sum(s2, axis=1, keepdims=True), (MINE, 128)),
        )

    def iteration(_, t):
        s1, s2 = sums(t)
        left, right = jnp.abs(-h - t), jnp.abs(h - t)
        nearest = jnp.where(last, left, jnp.minimum(left, right))
        return limited(t, s1, s2, nearest)

    t = lax.fori_loop(0, ITERS, iteration, t)
    norm = lax.rsqrt(sums(t)[1])
    index = lax.broadcasted_iota(jnp.int32, (MINE, 128), 0)
    lanes = lax.broadcasted_iota(jnp.int32, (MINE, 128), 1)
    out = jnp.where(lanes == index, c, 0.0)
    out = out + jnp.where(lanes == index + 16, t, 0.0)
    out = out + jnp.where(lanes == index + 32, norm, 0.0)
    tbl_ref[...] = jnp.sum(out, axis=0, keepdims=True)

    table = jnp.concatenate([*pieces(p_ref[...]), *pieces(w_ref[...])], axis=1)
    half = lax.div(col, 4)
    first = lax.rem(col, 4) * 512
    for q in range(4):
        both = cp_ref[:, pl.ds(pl.multiple_of(first + q * 128, 128), 128)]
        idx = jnp.where(half == 0, both[0:1, :], both[1:2, :])
        tile = lax.broadcasted_iota(jnp.int32, (TILES, 128), 0)
        onehot = jnp.where(tile == (idx >> 7), 1.0, 0.0).astype(BF16)
        got = lax.dot_general(table, onehot, (((0,), (0,)), ((), ())), preferred_element_type=F32)
        pick = lax.broadcasted_iota(jnp.int32, (128, 128), 0) == (idx & 127)
        for what in range(2):
            full = got[what * 384 : what * 384 + 128]
            full = full + got[what * 384 + 128 : what * 384 + 256]
            full = full + got[what * 384 + 256 : what * 384 + 384]
            pw_ref[what * 4 + q : what * 4 + q + 1, :] = jnp.sum(
                jnp.where(pick, full, 0.0), axis=0, keepdims=True
            )


def panel_roots(chosen, poles, weights, offsets, column_pole):
    return pl.pallas_call(
        panel_roots_kernel,
        name="panel_roots",
        out_shape=(jax.ShapeDtypeStruct((1, 128), F32), jax.ShapeDtypeStruct((8, 128), F32)),
        in_specs=[pl.BlockSpec(memory_space=pltpu.SMEM)] + [vmem()] * 4,
        out_specs=(vmem(),) * 2,
        scratch_shapes=[VMEM((TILES, 128), F32)] + [VMEM((MINE, 128), F32)] * 4,
        cost_estimate=pl.CostEstimate(flops=30_000_000, bytes_accessed=1 << 20, transcendentals=4_000_000),
    )(chosen, poles, weights, offsets, column_pole)


def share_kernel(tbl_ref, pw_ref, all_tbl, all_pw, mine, ts, tr, ws, wr, us, ur, ls):
    row, col = lax.axis_index("row"), lax.axis_index("col")
    own = [
        pltpu.make_async_copy(tbl_ref, mine.at[col], ls.at[0]),
        pltpu.make_async_copy(pw_ref, all_pw.at[col], ls.at[1]),
    ]
    for c in own:
        c.start()
    greet(row, col)
    a = spread(tbl_ref, mine, "col", COLS, col, ts, tr)
    b = spread(pw_ref, all_pw, "col", COLS, col, ws, wr)
    own[0].wait()
    collect(a, tbl_ref, mine, "col", COLS, col, ts, tr)
    last = pltpu.make_async_copy(mine, all_tbl.at[row], ls.at[2])
    last.start()
    c = spread(mine, all_tbl, "row", ROWS, row, us, ur)
    collect(b, pw_ref, all_pw, "col", COLS, col, ws, wr)
    own[1].wait()
    collect(c, mine, all_tbl, "row", ROWS, row, us, ur)
    last.wait()


def share(tbl, pw):
    return pl.pallas_call(
        share_kernel,
        name="share",
        out_shape=(
            jax.ShapeDtypeStruct((ROWS, COLS, 1, 128), F32),
            jax.ShapeDtypeStruct((COLS, 8, 128), F32),
        ),
        in_specs=[vmem()] * 2,
        out_specs=(vmem(),) * 2,
        scratch_shapes=[VMEM((COLS, 1, 128), F32), dma(7), dma(7), dma(7), dma(7), dma(15), dma(15), dma(3)],
        compiler_params=pltpu.CompilerParams(collective_id=1, has_side_effects=True),
    )(tbl, pw)


KB = 256


def product_kernel(tbl_ref, pw_ref, e_ref, *refs):
    outs, (cauchy, acc) = refs[:8], refs[8:]
    row = lax.axis_index("row")
    z, x = lax.div(row, 4), lax.rem(row, 4)
    half, block = pl.program_id(0), pl.program_id(1)
    lanes = lax.broadcasted_iota(jnp.int32, (128, 128), 1)

    def column(which):
        picked = jnp.where(lanes == which, tbl_ref[...], 0.0)
        return jnp.broadcast_to(jnp.sum(picked, axis=1, keepdims=True), (128, 128))

    for sub in range(KB // 128):
        k = block * (KB // 128) + sub
        center, offset, norm = column(k), column(16 + k), column(32 + k)
        for tile in range(16):
            pole = pw_ref[half * 4 + tile // 4, tile % 4 : tile % 4 + 1, :]
            weight = pw_ref[half * 4 + tile // 4, 4 + tile % 4 : 5 + tile % 4, :]
            inverse = 1.0 / ((pole - center) - offset)
            cauchy[sub * 128 : sub * 128 + 128, tile * 128 : tile * 128 + 128] = (
                (weight * inverse) * norm
            ).astype(BF16)
    acc[...] = lax.dot_general(
        e_ref[0], cauchy[...], (((1,), (1,)), ((), ())), preferred_element_type=F32
    )

    @pl.when(half == 0)
    def _():
        for j in range(4):
            to = lax.rem(z + j, 4)
            outs[j][...] = acc[pl.ds(pl.multiple_of(to * 192, 192), 192), :].astype(outs[j].dtype)

    @pl.when(half == 1)
    def _():
        for j in range(4):
            to = lax.rem(x + j, 4)
            for s in range(4):
                outs[4 + j][s * 48 : s * 48 + 48, :] = acc[
                    pl.ds(pl.multiple_of(s * 192 + to * 48, 48), 48), :
                ].astype(outs[4 + j].dtype)


def product(tbl, pw, halves):
    steps = PANEL // KB

    def first(h, k):
        return (0, jnp.where(h == 0, k, steps - 1))

    def second(h, k):
        return (0, jnp.where(h == 0, 0, k))

    kinds = [F32, BF16, BF16, BF16] * 2
    return pl.pallas_call(
        product_kernel,
        name="product",
        grid=(2, steps),
        out_shape=tuple(jax.ShapeDtypeStruct((192, PANEL), k) for k in kinds),
        in_specs=[
            pl.BlockSpec((128, 128), lambda h, k: (0, 0)),
            pl.BlockSpec((COLS, 8, 128), lambda h, k: (0, 0, 0)),
            pl.BlockSpec((1, 768, 2048), lambda h, k: (h, 0, 0)),
        ],
        out_specs=tuple([pl.BlockSpec((192, KB), first)] * 4 + [pl.BlockSpec((192, KB), second)] * 4),
        scratch_shapes=[VMEM((KB, 2048), BF16), VMEM((768, KB), F32)],
        cost_estimate=pl.CostEstimate(flops=13_000_000_000, bytes_accessed=20 << 20, transcendentals=8_000_000),
    )(tbl, pw, halves)


SUB = 64


def roots_kernel(p_ref, w_ref, c_ref, t_ref, out_ref, w2, pd, xs, a1, a2):
    row, col = lax.axis_index("row"), lax.axis_index("col")
    first = col * 64 + row * 4
    w2[...] = w_ref[...] * w_ref[...]
    lane = lax.broadcasted_iota(jnp.int32, (1, 128), 1)

    def block(b, _):
        c, t = c_ref[pl.ds(b, 1), :], t_ref[pl.ds(b, 1), :]
        own = p_ref[pl.ds(first + b, 1), :]
        origin = own[:, 64:65]
        pd[...] = p_ref[...] - origin
        x = (c - origin) + t
        xs[...] = jnp.broadcast_to(x, (128, 128)).T
        for sub in range(128 // SUB):
            x_sub = xs[sub * SUB : sub * SUB + SUB, :]

            def step(s, carry):
                s1, s2 = carry
                for k in range(4):
                    pole = pd[pl.ds(s * 4 + k, 1), :]
                    wsq = w2[pl.ds(s * 4 + k, 1), :]
                    inverse = 1.0 / (pole - x_sub)
                    weighted = wsq * inverse
                    s1 = s1 + weighted
                    s2 = s2 + weighted * inverse
                return s1, s2

            zero = jnp.zeros((SUB, 128), F32)
            s1, s2 = lax.fori_loop(0, TILES // 4, step, (zero, zero))
            a1[sub * SUB : sub * SUB + SUB, :] = s1
            a2[sub * SUB : sub * SUB + SUB, :] = s2
        s1 = jnp.sum(a1[...].T, axis=0, keepdims=True)
        s2 = jnp.sum(a2[...].T, axis=0, keepdims=True)
        h = c - own
        left, right = jnp.abs(-h - t), jnp.abs(h - t)
        last = (first + b) * 128 + lane == N - 1
        nearest = jnp.where(last, left, jnp.minimum(left, right))
        out_ref[pl.ds(b, 1), :] = limited(t, s1, s2, nearest)
        return 0

    lax.fori_loop(0, 4, block, 0)


def roots(poles, weights, centers, offsets):
    return pl.pallas_call(
        roots_kernel,
        name="roots",
        out_shape=jax.ShapeDtypeStruct((4, 128), F32),
        in_specs=[vmem()] * 4,
        out_specs=vmem(),
        scratch_shapes=[VMEM((TILES, 128), F32)] * 2 + [VMEM((128, 128), F32)] * 3,
        cost_estimate=pl.CostEstimate(flops=25_000_000_000, bytes_accessed=1 << 20, transcendentals=33_000_000),
    )(poles, weights, centers, offsets)


def finish_kernel(t_ref, out_ref, ts, tr, ls):
    row = lax.axis_index("row")
    own = pltpu.make_async_copy(t_ref, out_ref.at[row], ls.at[0])
    own.start()
    barrier = pltpu.get_barrier_semaphore()
    for j in range(1, ROWS):
        pl.semaphore_signal(barrier, inc=1, device_id={"row": lax.rem(row + j, ROWS)}, device_id_type=MESH)
    pl.semaphore_wait(barrier, ROWS - 1)
    a = spread(t_ref, out_ref, "row", ROWS, row, ts, tr)
    collect(a, t_ref, out_ref, "row", ROWS, row, ts, tr)
    own.wait()


def finish(t):
    return pl.pallas_call(
        finish_kernel,
        name="finish",
        out_shape=jax.ShapeDtypeStruct((ROWS, 4, 128), F32),
        in_specs=[vmem()],
        out_specs=vmem(),
        scratch_shapes=[dma(15), dma(15), dma(1)],
        compiler_params=pltpu.CompilerParams(collective_id=2, has_side_effects=True),
    )(t)


def along(j, first):
    pairs = []
    for z in range(4):
        for x in range(4):
            to = ((z + j) % 4, x) if first else (z, (x + j) % 4)
            pairs.append((z * 4 + x, to[0] * 4 + to[1]))
    return pairs


def on_device(pole_values, weights, centers, offsets, chosen, column_pole, eigen_blocks):
    row = lax.axis_index("row")
    z, x = lax.div(row, 4), lax.rem(row, 4)
    all_p, all_w, all_o = gather_all(pole_values, weights, offsets)
    all_p, all_w, all_o = (a.reshape(TILES, 128) for a in (all_p, all_w, all_o))
    tbl, pw = share(*panel_roots(chosen, all_p, all_w, all_o, column_pole))
    halves = jnp.transpose(eigen_blocks, (1, 0, 2))
    blocks = product(tbl.reshape(128, 128), pw, halves)

    def moved(block, j, first):
        return lax.ppermute(block, "row", along(j, first))

    got = [[moved(blocks[4 * half + j], j, half == 0) for j in (1, 2, 3)] for half in range(2)]

    my_centers = lax.dynamic_slice_in_dim(centers.reshape(64, 128), row * 4, 4)
    t = lax.dynamic_slice_in_dim(offsets.reshape(64, 128), row * 4, 4)
    t, blocks = lax.optimization_barrier((t, blocks))
    t = roots(all_p, all_w, my_centers, t)
    t = roots(all_p, all_w, my_centers, t)
    got, t = lax.optimization_barrier((got, t))
    panels, sent = [], []
    for half in range(2):
        total = blocks[4 * half]
        for g in got[half]:
            total = total + g.astype(F32)
        total = total.reshape(4, 48, PANEL)
        me = x if half == 0 else z
        sent.append([
            moved(lax.dynamic_index_in_dim(total, lax.rem(me + j, 4), 0, False).astype(BF16), j, half == 1)
            for j in (1, 2, 3)
        ])
        panels.append(lax.dynamic_index_in_dim(total, me, 0, False))
    t = roots(all_p, all_w, my_centers, t)
    sent, t = lax.optimization_barrier((sent, t))
    offset_now = finish(t).reshape(8192)
    for half in range(2):
        for g in sent[half]:
            panels[half] = panels[half] + g.astype(F32)
    return offset_now, jnp.stack(panels, axis=1)


def solution(mesh):
    placed = (P("row"), P("row"), P("col"), P("col"), P(), P(None, "row"), P("col", None, "row"))
    return jax.shard_map(
        on_device,
        mesh=mesh,
        in_specs=placed,
        out_specs=(P("col"), P(("col", "row"), None, None)),
        check_vma=False,
    )
```

time: 558 us -> 227 us (0.41)
  Pallas kernels: 0 us -> 187 us
  waiting for transfers between devices: 173 us -> 0.03 us
  other arithmetic: 155 us -> 5.32 us
  local copies, waits for them, and re-layouts: 119 us -> 15.6 us
  blocking collectives: 60.3 us -> 0 us
  matrix products: 27 us -> 0 us
  between operations: 15 us -> 0.78 us
  starting transfers between devices: 4.98 us -> 17.1 us
    pallas_call x0 -> x8, Pallas kernels: none -> 187 us  [the longest x3 111 us: roots(): pl.pallas_call(roots_kernel, name='roots', out_shape=jax.ShapeDtypeStruct...]
    unnamed x2 -> x0, waiting for transfers between devices: 173 us -> none
    reduce_sum x80 -> x0, other arithmetic: 143 us -> none  [per_block(): jnp.sum(weighted * inverse, axis=1)]
    gather x6 -> x0, local copies, waits for them, and re-layouts: 70.7 us -> none  [the longest x2 23.6 us: on_device(): all_weights[pole_index]]
    all_gather x2 -> x0, blocking collectives: 38.7 us -> none  [gather_turned(): filled = lax.all_gather(both, axis, axis=0, tiled=True)]
    dot_general x2 -> x0, matrix products: 27 us -> none  [on_device(): jnp.dot(eigen_blocks[:, half_index, :], cauchy_halves[half_index], prefer...]
    psum x2 -> x0, blocking collectives: 21.6 us -> none  [by_axis(): shard = lax.psum(shard, axis)]
    another operation x10 -> x0, local copies, waits for them, and re-layouts: 19.4 us -> none  [the longest x1 19.4 us: on_device(): jnp.stack([jnp.dot(eigen_blocks[:, half_index, :], cauchy_halves[half_ind...]
  transfers between devices with their start and end apart: 2 -> 12, of which waited for: 1 -> 0; matrix products, arithmetic and copies ran while one was open for 11% -> 2% of each run, Pallas kernels for 0% -> 49%
where the time goes in v1:
time: 227 us; the launch traced here: 226 us
  Pallas kernels  187 us (82%)
  starting transfers between devices  17.1 us (8%)
  local copies, waits for them, and re-layouts  15.6 us (7%)
  other arithmetic  5.32 us (2%)
    pallas_call x3, Pallas kernels, roots(): pl.pallas_call(roots_kernel, name='roots', out_shape=jax.ShapeDtypeStruct...  111 us
    pallas_call x1, Pallas kernels, product(): pl.pallas_call(product_kernel, name='product', grid=(2, steps), out_shape...  26 us
    ppermute x12, starting transfers between devices, moved(): return lax.ppermute(block, 'row', along(j, first))  17.1 us
    pallas_call x1, Pallas kernels, gather_all(): pl.pallas_call(gather_kernel, name='gather_all', out_shape=(jax.ShapeDtyp...  17.1 us
    pallas_call x1, Pallas kernels, share(): pl.pallas_call(share_kernel, name='share', out_shape=(jax.ShapeDtypeStruc...  13.5 us
    unnamed x17, local copies, waits for them, and re-layouts  12.1 us
    pallas_call x1, Pallas kernels, finish(): pl.pallas_call(finish_kernel, name='finish', out_shape=jax.ShapeDtypeStru...  10.3 us
    pallas_call x1, Pallas kernels, panel_roots(): pl.pallas_call(panel_roots_kernel, name='panel_roots', out_shape=(jax.Sha...  9.39 us
  transfers between devices with their start and end apart: 12, of which 0 were waited for; matrix products, arithmetic and copies ran while one was open for 2% of the time, Pallas kernels for 49%

profile of v1, /device:TPU:8, one launch (start us, length us, event | category | flops | bytes accessed | tf_op | source)
XLA Modules:
  0.0 225.7 jit_solution(10354898376819474320)
XLA Ops:
  0.6 8.3 %copy.13 = bf16[768,2,2048]{2,0,1:T(8,128)(2,1)} copy(bf16[768,2,2048]{2,1,0:T(2,128)(2,1)} %param.13) | data formatting | bytes 12582912 | tf_op args[6]
  9.0 17.1 %gather_all.1 = (f32[16,32,128]{2,1,0:T(8,128)}, f32[16,32,128]{2,1,0:T(8,128)}, f32[8,64,128]{2,1,0:T(8,128)}) custom-call(f32[32,128]{1,0:T(8,128)} %bitcast.55, f32[32,128]{1,0:T(8,128)} %bitcast.56, f32[64,128]{1,0:T(8,128)} %bitcast.53), custom_call_target="tpu_custom_call" | custom-call | tf_op jit(solution)/shard_map/gather_all/pallas_call | solution.py:90
  26.1 9.4 %panel_roots.1 = (f32[1,128]{1,0:T(1,128)}, f32[8,128]{1,0:T(8,128)}) custom-call(s32[2048]{0:T(1024)} %ch_ref.1, f32[512,128]{1,0:T(8,128)} %bitcast.57, f32[512,128]{1,0:T(8,128)} %bitcast.61, f32[512,128]{1,0:T(8,128)} %bitcast.65, s32[2,2048]{1,0:T(2,128)} %cp_ref.1), custom_call_target="tpu_custom_call" | custom-call | flops 30000000 | bytes 1048576 | tf_op jit(solution)/shard_map/panel_roots/pallas_call | solution.py:193
  35.4 13.5 %share.1 = (f32[16,8,1,128]{3,2,1,0:T(1,128)}, f32[8,8,128]{2,1,0:T(8,128)}) custom-call(f32[1,128]{1,0:T(1,128)} %get-tuple-element.37.tbl_ref, f32[8,128]{1,0:T(8,128)} %get-tuple-element.38.pw_ref), custom_call_target="tpu_custom_call" | custom-call | tf_op jit(solution)/shard_map/share/pallas_call | solution.py:227
  48.9 26.0 %product.1 = (f32[192,2048]{1,0:T(8,128)}, bf16[192,2048]{1,0:T(8,128)(2,1)}, bf16[192,2048]{1,0:T(8,128)(2,1)}, bf16[192,2048]{1,0:T(8,128)(2,1)}, f32[192,2048...) custom-call(f32[128,128]{1,0:T(8,128)} %bitcast.66, ...), custom_call_target="tpu_custom_call" | custom-call | flops 12999999488 | bytes 20971520 | tf_op jit(solution)/shard_map/product/pallas_call | solution.py:295
  75.5 3.0 %collective-permute-start.1 = (bf16[192,2048]{1,0:T(8,128)(2,1)}, bf16[192,2048]{1,0:T(8,128)(2,1)S(1)}, u32[]{:S(2)}, u32[]{:S(2)}) collective-permute-start(bf16[192,2048]{1,0:T(8,128)(2,1)} %get-tuple-element.43), channel_id=1, source_target_pairs={{0,64},{8,72},{16,80},{24,88},{32,96},{40,104},{48,112},{56,120},{... | collective-permute-start | bytes 2359304 | tf_op jit(solution)/shard_map/ppermute | solution.py:413
  78.5 1.2 collective-permute-start.2
  80.4 2.8 %collective-permute-start.4 = (bf16[192,2048]{1,0:T(8,128)(2,1)}, bf16[192,2048]{1,0:T(8,128)(2,1)}, u32[]{:S(2)}, u32[]{:S(2)}) collective-permute-start(bf16[192,2048]{1,0:T(8,128)(2,1)} %get-tuple-element.47), channel_id=1, source_target_pairs={{0,16},{8,24},{16,0},{24,8},{32,48},{40,56},{48,32},{56,40},{64,80... | collective-permute-start | bytes 2359304 | tf_op jit(solution)/shard_map/ppermute | solution.py:413
  83.3 1.3 constant_dynamic-slice_fusion.1.t_ref
  85.1 36.9 %roots.3.t_ref = f32[4,128]{1,0:T(4,128)} custom-call(f32[512,128]{1,0:T(8,128)} %bitcast.58, f32[512,128]{1,0:T(8,128)} %bitcast.62, f32[4,128]{1,0:T(4,128)} %constant_dynamic-slice_fusion.c_ref, f32[4,128]{1,0:T(4,128)} %constant_dynamic-slice_fusion.1.t_ref), custom_call_target="tpu_custom_call" | custom-call | flops 24999999488 | bytes 1048576 | tf_op jit(solution)/shard_map/roots/pallas_call | solution.py:358
  122.0 1.4 collective-permute-start.5
  123.4 36.9 %roots.4.t_ref = f32[4,128]{1,0:T(4,128)} custom-call(f32[512,128]{1,0:T(8,128)} %bitcast.59, f32[512,128]{1,0:T(8,128)} %bitcast.63, f32[4,128]{1,0:T(4,128)} %constant_dynamic-slice_fusion.c_ref, f32[4,128]{1,0:T(4,128)} %roots.3.t_ref), custom_call_target="tpu_custom_call" | custom-call | flops 24999999488 | bytes 1048576 | tf_op jit(solution)/shard_map/roots/pallas_call | solution.py:358
  160.3 0.8 copy-done.5
  161.1 2.2 convert_add_fusion
  164.2 1.5 collective-permute-start.10
  165.7 2.1 collective-permute-start.11
  167.7 1.6 convert_add_fusion.1
  170.8 1.1 collective-permute-start.7
  172.0 2.1 collective-permute-start.8
  174.1 36.9 %roots.5.t_ref = f32[4,128]{1,0:T(4,128)} custom-call(f32[512,128]{1,0:T(8,128)} %bitcast.60, f32[512,128]{1,0:T(8,128)} %bitcast.64, f32[4,128]{1,0:T(4,128)} %constant_dynamic-slice_fusion.c_ref, f32[4,128]{1,0:T(4,128)} %roots.4.t_ref), custom_call_target="tpu_custom_call" | custom-call | flops 24999999488 | bytes 1048576 | tf_op jit(solution)/shard_map/roots/pallas_call | solution.py:358
  211.0 1.5 fusion.2
  212.5 1.5 copy.11
  214.0 10.3 %finish.1 = f32[16,4,128]{2,1,0:T(4,128)} custom-call(f32[4,128]{1,0:T(4,128)} %roots.5.t_ref), custom_call_target="tpu_custom_call" | custom-call | tf_op jit(solution)/shard_map/finish/pallas_call | solution.py:383
  224.3 1.4 copy.15
  (33 shorter events, 4.3 us)
Async XLA Ops:
  0.6 83.9 %copy-start = (f32[8192]{0:T(1024)S(1)}, f32[8192]{0:T(1024)}, u32[]{:S(2)}) copy-start(f32[8192]{0:T(1024)} %param.9) | copy-start | bytes 98308
  74.9 47.0 %collective-permute-start = (bf16[192,2048]{1,0:T(8,128)(2,1)}, bf16[192,2048]{1,0:T(8,128)(2,1)S(1)}, u32[]{:S(2)}, u32[]{:S(2)}) collective-permute-start(bf16[192,2048]{1,0:T(8,128)(2,1)} %get-tuple-element.42), channel_id=1, source_target_pairs={{0,32},{8,40},{16,48},{24,56},{32,64},{40,72},{48,80},{56,88},{64,... | collective-permute-start | bytes 2359304 | tf_op jit(solution)/shard_map/ppermute | solution.py:413
  75.5 84.7 %collective-permute-start.1 = (bf16[192,2048]{1,0:T(8,128)(2,1)}, bf16[192,2048]{1,0:T(8,128)(2,1)S(1)}, u32[]{:S(2)}, u32[]{:S(2)}) collective-permute-start(bf16[192,2048]{1,0:T(8,128)(2,1)} %get-tuple-element.43), channel_id=1, source_target_pairs={{0,64},{8,72},{16,80},{24,88},{32,96},{40,104},{48,112},{56,120},{... | collective-permute-start | bytes 2359304 | tf_op jit(solution)/shard_map/ppermute | solution.py:413
  78.5 81.7 %collective-permute-start.2 = (bf16[192,2048]{1,0:T(8,128)(2,1)}, bf16[192,2048]{1,0:T(8,128)(2,1)}, u32[]{:S(2)}, u32[]{:S(2)}) collective-permute-start(bf16[192,2048]{1,0:T(8,128)(2,1)} %get-tuple-element.44), channel_id=1, source_target_pairs={{0,96},{8,104},{16,112},{24,120},{32,0},{40,8},{48,16},{56,24},{64... | collective-permute-start | bytes 2359304 | tf_op jit(solution)/shard_map/ppermute | solution.py:413
  79.7 80.5 %collective-permute-start.3 = (bf16[192,2048]{1,0:T(8,128)(2,1)}, bf16[192,2048]{1,0:T(8,128)(2,1)}, u32[]{:S(2)}, u32[]{:S(2)}) collective-permute-start(bf16[192,2048]{1,0:T(8,128)(2,1)} %get-tuple-element.46), channel_id=1, source_target_pairs={{0,8},{8,16},{16,24},{24,0},{32,40},{40,48},{48,56},{56,32},{64,72... | collective-permute-start | bytes 2359304 | tf_op jit(solution)/shard_map/ppermute | solution.py:413
  80.4 79.8 %collective-permute-start.4 = (bf16[192,2048]{1,0:T(8,128)(2,1)}, bf16[192,2048]{1,0:T(8,128)(2,1)}, u32[]{:S(2)}, u32[]{:S(2)}) collective-permute-start(bf16[192,2048]{1,0:T(8,128)(2,1)} %get-tuple-element.47), channel_id=1, source_target_pairs={{0,16},{8,24},{16,0},{24,8},{32,48},{40,56},{48,32},{56,40},{64,80... | collective-permute-start | bytes 2359304 | tf_op jit(solution)/shard_map/ppermute | solution.py:413
  122.0 39.2 %copy-start.2 = (f32[192,2048]{1,0:T(8,128)S(1)}, f32[192,2048]{1,0:T(8,128)}, u32[]{:S(2)}) copy-start(f32[192,2048]{1,0:T(8,128)} %get-tuple-element.54) | copy-start | bytes 4718596
  122.0 38.3 %copy-start.3 = (bf16[192,2048]{1,0:T(8,128)(2,1)}, bf16[192,2048]{1,0:T(8,128)(2,1)S(1)}, u32[]{:S(2)}) copy-start(bf16[192,2048]{1,0:T(8,128)(2,1)S(1)} %collective-permute-done) | copy-start | bytes 2359300
  122.0 39.1 %collective-permute-start.5 = (bf16[192,2048]{1,0:T(8,128)(2,1)}, bf16[192,2048]{1,0:T(8,128)(2,1)}, u32[]{:S(2)}, u32[]{:S(2)}) collective-permute-start(bf16[192,2048]{1,0:T(8,128)(2,1)} %get-tuple-element.48), channel_id=1, source_target_pairs={{0,24},{8,0},{16,8},{24,16},{32,56},{40,32},{48,40},{56,48},{64,88... | collective-permute-start | bytes 2359304 | tf_op jit(solution)/shard_map/ppermute | solution.py:413
  160.2 0.9 copy-start.5
  161.1 6.6 %copy-start.1 = (f32[192,2048]{1,0:T(8,128)S(1)}, f32[192,2048]{1,0:T(8,128)}, u32[]{:S(2)}) copy-start(f32[192,2048]{1,0:T(8,128)} %get-tuple-element.49) | copy-start | bytes 4718596
  161.1 6.6 %copy-start.6 = (bf16[192,2048]{1,0:T(8,128)(2,1)S(1)}, bf16[192,2048]{1,0:T(8,128)(2,1)}, u32[]{:S(2)}) copy-start(bf16[192,2048]{1,0:T(8,128)(2,1)} %copy-done.5) | copy-start | bytes 2359300
  163.3 4.4 %copy-start.4 = (bf16[192,2048]{1,0:T(8,128)(2,1)S(1)}, bf16[192,2048]{1,0:T(8,128)(2,1)}, u32[]{:S(2)}) copy-start(bf16[192,2048]{1,0:T(8,128)(2,1)} %copy-done.3) | copy-start | bytes 2359300
  164.2 7.8 %collective-permute-start.10 = (bf16[48,2048]{1,0:T(8,128)(2,1)S(1)}, bf16[48,2048]{1,0:T(8,128)(2,1)S(1)}, u32[]{:S(2)}, u32[]{:S(2)}) collective-permute-start(bf16[48,2048]{1,0:T(8,128)(2,1)S(1)} %get-tuple-element.69), channel_id=1, source_target_pairs={{0,64},{8,72},{16,80},{24,88},{32,96},{40,104},{48,112},{56,120},{... | collective-permute-start | bytes 589832 | tf_op jit(solution)/shard_map/ppermute | solution.py:413
  165.7 45.3 %collective-permute-start.11 = (bf16[48,2048]{1,0:T(8,128)(2,1)}, bf16[48,2048]{1,0:T(8,128)(2,1)}, u32[]{:S(2)}, u32[]{:S(2)}) collective-permute-start(bf16[48,2048]{1,0:T(8,128)(2,1)} %get-tuple-element.68), channel_id=1, source_target_pairs={{0,96},{8,104},{16,112},{24,120},{32,0},{40,8},{48,16},{56,24},{64... | collective-permute-start | bytes 589832 | tf_op jit(solution)/shard_map/ppermute | solution.py:413
  167.7 43.2 %collective-permute-start.9 = (bf16[48,2048]{1,0:T(8,128)(2,1)}, bf16[48,2048]{1,0:T(8,128)(2,1)}, u32[]{:S(2)}, u32[]{:S(2)}) collective-permute-start(bf16[48,2048]{1,0:T(8,128)(2,1)} %get-tuple-element.70), channel_id=1, source_target_pairs={{0,32},{8,40},{16,48},{24,56},{32,64},{40,72},{48,80},{56,88},{64,... | collective-permute-start | bytes 589832 | tf_op jit(solution)/shard_map/ppermute | solution.py:413
  170.2 40.8 %collective-permute-start.6 = (bf16[48,2048]{1,0:T(8,128)(2,1)}, bf16[48,2048]{1,0:T(8,128)(2,1)}, u32[]{:S(2)}, u32[]{:S(2)}) collective-permute-start(bf16[48,2048]{1,0:T(8,128)(2,1)} %get-tuple-element.73), channel_id=1, source_target_pairs={{0,8},{8,16},{16,24},{24,0},{32,40},{40,48},{48,56},{56,32},{64,72... | collective-permute-start | bytes 589832 | tf_op jit(solution)/shard_map/ppermute | solution.py:413
  170.8 40.1 %collective-permute-start.7 = (bf16[48,2048]{1,0:T(8,128)(2,1)}, bf16[48,2048]{1,0:T(8,128)(2,1)}, u32[]{:S(2)}, u32[]{:S(2)}) collective-permute-start(bf16[48,2048]{1,0:T(8,128)(2,1)} %get-tuple-element.72), channel_id=1, source_target_pairs={{0,16},{8,24},{16,0},{24,8},{32,48},{40,56},{48,32},{56,40},{64,80... | collective-permute-start | bytes 589832 | tf_op jit(solution)/shard_map/ppermute | solution.py:413
  172.0 39.0 %collective-permute-start.8 = (bf16[48,2048]{1,0:T(8,128)(2,1)}, bf16[48,2048]{1,0:T(8,128)(2,1)}, u32[]{:S(2)}, u32[]{:S(2)}) collective-permute-start(bf16[48,2048]{1,0:T(8,128)(2,1)} %get-tuple-element.71), channel_id=1, source_target_pairs={{0,24},{8,0},{16,8},{24,16},{32,56},{40,32},{48,40},{56,48},{64,88... | collective-permute-start | bytes 589832 | tf_op jit(solution)/shard_map/ppermute | solution.py:413

commit v2 on v1

--- a/solution.py
+++ b/solution.py
@@ -308,61 +308,132 @@
     )(tbl, pw, halves)
 
 
-SUB = 64
-
-
-def roots_kernel(p_ref, w_ref, c_ref, t_ref, out_ref, w2, pd, xs, a1, a2):
-    row, col = lax.axis_index("row"), lax.axis_index("col")
-    first = col * 64 + row * 4
-    w2[...] = w_ref[...] * w_ref[...]
+CHAIN = 64
+WINDOW = 5
+PAIRS = TILES // 2
+
+
+def weight_tables(w_ref, q):
+    w = jnp.concatenate([w_ref[pl.ds(2 * q, 1), :], w_ref[pl.ds(2 * q + 1, 1), :]], axis=1)
+    w = jnp.broadcast_to(w, (8, 256))
+    first = w.astype(BF16)
+    exact = w * w / first.astype(F32)
+    lane = lax.broadcasted_iota(jnp.int32, (8, 256), 1)
+    turn = lax.rem(lane * 79 + 37, 128).astype(F32) / 128.0 + (1.0 / 256.0 - 0.5)
+    step = jnp.where(exact >= 0.25, 2.0**-9, 2.0**-10)
+    return first, (exact + turn * step).astype(BF16)
+
+
+def root_block(b, first, p_ref, w_ref, c_ref, t_ref, out_ref, wa, wv, pd, pb, xs, a1, a2):
     lane = lax.broadcasted_iota(jnp.int32, (1, 128), 1)
-
-    def block(b, _):
-        c, t = c_ref[pl.ds(b, 1), :], t_ref[pl.ds(b, 1), :]
-        own = p_ref[pl.ds(first + b, 1), :]
-        origin = own[:, 64:65]
-        pd[...] = p_ref[...] - origin
-        x = (c - origin) + t
-        xs[...] = jnp.broadcast_to(x, (128, 128)).T
-        for sub in range(128 // SUB):
-            x_sub = xs[sub * SUB : sub * SUB + SUB, :]
-
-            def step(s, carry):
-                s1, s2 = carry
-                for k in range(4):
-                    pole = pd[pl.ds(s * 4 + k, 1), :]
-                    wsq = w2[pl.ds(s * 4 + k, 1), :]
-                    inverse = 1.0 / (pole - x_sub)
+    c = c_ref[pl.ds(b, 1), :]
+    own = p_ref[pl.ds(first + b, 1), :]
+    origin = own[:, 64:65]
+    start = jnp.clip(lax.div(first + b, 2) - WINDOW // 2, 0, PAIRS - WINDOW)
+    pd[...] = p_ref[...] - origin
+
+    def fill(q, _):
+        pole = jnp.concatenate([pd[pl.ds(2 * q, 1), :], pd[pl.ds(2 * q + 1, 1), :]], axis=1)
+        pb[q] = jnp.broadcast_to(pole, (8, 256)).astype(BF16)
+        return 0
+
+    lax.fori_loop(0, PAIRS, fill, 0, unroll=8)
+    for k in range(WINDOW):
+        wa[start + k] = jnp.zeros((8, 256), BF16)
+        wv[start + k] = jnp.zeros((8, 256), BF16)
+        pb[start + k] = jnp.full((8, 256), 8192.0, BF16)
+    one = jnp.ones((8, 256), BF16)
+    h = c - own
+    last = (first + b) * 128 + lane == N - 1
+
+    def iteration(_, t):
+        xs[...] = jnp.broadcast_to((c - origin) + t, (128, 128)).T
+
+        def groups(g, _):
+            x_g = [xs[pl.ds(pl.multiple_of(g * 16 + 8 * k, 8), 8), :] for k in range(2)]
+            x_w = [jnp.concatenate([v, v], axis=1).astype(BF16) for v in x_g]
+
+            def chain(s, carry):
+                sums = [[None, None], [None, None]]
+
+                def add(k, scaled, v):
+                    one_ = scaled.astype(F32) * v.astype(F32)
+                    two_ = scaled.astype(F32) * scaled.astype(F32)
+                    sums[k][0] = one_ if sums[k][0] is None else sums[k][0] + one_
+                    sums[k][1] = two_ if sums[k][1] is None else sums[k][1] + two_
+
+                for i in range(0, CHAIN, 2):
+                    q = s * CHAIN + i
+                    for k in range(2):
+                        a, d = pb[q] - x_w[k], pb[q + 1] - x_w[k]
+                        inverse = one / (a * d)
+                        add(k, wa[q] * (d * inverse), wv[q])
+                        add(k, wa[q + 1] * (a * inverse), wv[q + 1])
+                return tuple(tuple(c + s for c, s in zip(cs, ss)) for cs, ss in zip(carry, sums))
+
+            zero = jnp.zeros((8, 256), F32)
+            far = lax.fori_loop(0, PAIRS // CHAIN, chain, ((zero, zero), (zero, zero)))
+            near = [[f[:, :128] + f[:, 128:] for f in fs] for fs in far]
+            for i in range(2 * WINDOW):
+                pole = pd[pl.ds(2 * start + i, 1), :]
+                w = w_ref[pl.ds(2 * start + i, 1), :]
+                wsq = w * w
+                for k in range(2):
+                    inverse = 1.0 / (pole - x_g[k])
                     weighted = wsq * inverse
-                    s1 = s1 + weighted
-                    s2 = s2 + weighted * inverse
-                return s1, s2
-
-            zero = jnp.zeros((SUB, 128), F32)
-            s1, s2 = lax.fori_loop(0, TILES // 4, step, (zero, zero))
-            a1[sub * SUB : sub * SUB + SUB, :] = s1
-            a2[sub * SUB : sub * SUB + SUB, :] = s2
+                    near[k][0] = near[k][0] + weighted
+                    near[k][1] = near[k][1] + weighted * inverse
+            for k in range(2):
+                at = pl.ds(pl.multiple_of(g * 16 + 8 * k, 8), 8)
+                a1[at, :], a2[at, :] = near[k]
+            return 0
+
+        lax.fori_loop(0, 8, groups, 0)
         s1 = jnp.sum(a1[...].T, axis=0, keepdims=True)
         s2 = jnp.sum(a2[...].T, axis=0, keepdims=True)
-        h = c - own
         left, right = jnp.abs(-h - t), jnp.abs(h - t)
-        last = (first + b) * 128 + lane == N - 1
         nearest = jnp.where(last, left, jnp.minimum(left, right))
-        out_ref[pl.ds(b, 1), :] = limited(t, s1, s2, nearest)
+        return limited(t, s1, s2, nearest)
+
+    out_ref[pl.ds(b, 1), :] = lax.fori_loop(0, ITERS, iteration, t_ref[pl.ds(b, 1), :])
+    for k in range(WINDOW):
+        wa[start + k], wv[start + k] = weight_tables(w_ref, start + k)
+
+
+def roots_kernel(p_ref, w_ref, c_ref, t_ref, out_ref, wa, wv, *scratch):
+    row, col = lax.axis_index("row"), lax.axis_index("col")
+    first = col * 64 + row * 4 + (4 - t_ref.shape[0]) * FIRST_OF[t_ref.shape[0]]
+
+    def fill(q, _):
+        wa[q], wv[q] = weight_tables(w_ref, q)
         return 0
 
-    lax.fori_loop(0, 4, block, 0)
+    lax.fori_loop(0, PAIRS, fill, 0, unroll=4)
+
+    def block(b, _):
+        root_block(b, first, p_ref, w_ref, c_ref, t_ref, out_ref, wa, wv, *scratch)
+        return 0
+
+    lax.fori_loop(0, t_ref.shape[0], block, 0)
+
+
+FIRST_OF = {3: 0, 1: 1}
 
 
 def roots(poles, weights, centers, offsets):
+    blocks = offsets.shape[0]
     return pl.pallas_call(
         roots_kernel,
-        name="roots",
-        out_shape=jax.ShapeDtypeStruct((4, 128), F32),
+        name=f"roots{blocks}",
+        out_shape=jax.ShapeDtypeStruct((blocks, 128), F32),
         in_specs=[vmem()] * 4,
         out_specs=vmem(),
-        scratch_shapes=[VMEM((TILES, 128), F32)] * 2 + [VMEM((128, 128), F32)] * 3,
-        cost_estimate=pl.CostEstimate(flops=25_000_000_000, bytes_accessed=1 << 20, transcendentals=33_000_000),
+        scratch_shapes=[VMEM((PAIRS, 8, 256), BF16)] * 2
+        + [VMEM((TILES, 128), F32), VMEM((PAIRS, 8, 256), BF16)]
+        + [VMEM((128, 128), F32)] * 3,
+        cost_estimate=pl.CostEstimate(
+            flops=blocks * 12_000_000_000, bytes_accessed=1 << 20, transcendentals=33_000_000
+        ),
     )(poles, weights, centers, offsets)
 
 
@@ -417,9 +488,8 @@
     my_centers = lax.dynamic_slice_in_dim(centers.reshape(64, 128), row * 4, 4)
     t = lax.dynamic_slice_in_dim(offsets.reshape(64, 128), row * 4, 4)
     t, blocks = lax.optimization_barrier((t, blocks))
-    t = roots(all_p, all_w, my_centers, t)
-    t = roots(all_p, all_w, my_centers, t)
-    got, t = lax.optimization_barrier((got, t))
+    t_most = roots(all_p, all_w, my_centers[:3], t[:3])
+    got, t_most, t_rest = lax.optimization_barrier((got, t_most, t[3:]))
     panels, sent = [], []
     for half in range(2):
         total = blocks[4 * half]
@@ -432,7 +502,7 @@
             for j in (1, 2, 3)
         ])
         panels.append(lax.dynamic_index_in_dim(total, me, 0, False))
-    t = roots(all_p, all_w, my_centers, t)
+    t = jnp.concatenate([t_most, roots(all_p, all_w, my_centers[3:], t_rest)])
     sent, t = lax.optimization_barrier((sent, t))
     offset_now = finish(t).reshape(8192)
     for half in range(2):

time: 227 us -> 211 us (0.930)
  Pallas kernels: 187 us -> 142 us
  starting transfers between devices: 17.1 us -> 31.1 us
  waiting for transfers between devices: 0.03 us -> 11.4 us
  local copies, waits for them, and re-layouts: 15.6 us -> 18.1 us
    pallas_call x3 -> x2, Pallas kernels: 111 us -> 66.9 us  [roots(): pl.pallas_call(roots_kernel, name=f'roots{blocks}', out_shape=jax.ShapeDt...]
    ppermute x12, starting transfers between devices: 17.1 us -> 31.1 us  [moved(): return lax.ppermute(block, 'row', along(j, first))]
    ppermute x12, waiting for transfers between devices: 0.03 us -> 11.4 us  [moved(): return lax.ppermute(block, 'row', along(j, first))]
    slice x0 -> x2, local copies, waits for them, and re-layouts: none -> 2.47 us  [the longest x1 1.27 us: on_device(): got, t_most, t_rest = lax.optimization_barrier((got, t_most, t[3:]))]
    unnamed x17 -> x19, local copies, waits for them, and re-layouts: 12.1 us -> 12.1 us
  transfers between devices with their start and end apart: 12 -> 12, of which waited for: 0 -> 1; matrix products, arithmetic and copies ran while one was open for 2% -> 4% of each run, Pallas kernels for 49% -> 32%
where the time goes in v2:
time: 211 us; the launch traced here: 210 us
  Pallas kernels  142 us (67%)
  starting transfers between devices  31.1 us (15%)
  local copies, waits for them, and re-layouts  18.1 us (9%)
  waiting for transfers between devices  11.4 us (5%)
  other arithmetic  6.56 us (3%)
    pallas_call x2, Pallas kernels, roots(): pl.pallas_call(roots_kernel, name=f'roots{blocks}', out_shape=jax.ShapeDt...  66.9 us
    ppermute x12, starting transfers between devices, moved(): return lax.ppermute(block, 'row', along(j, first))  31.1 us
    pallas_call x1, Pallas kernels, product(): pl.pallas_call(product_kernel, name='product', grid=(2, steps), out_shape...  26 us
    pallas_call x1, Pallas kernels, gather_all(): pl.pallas_call(gather_kernel, name='gather_all', out_shape=(jax.ShapeDtyp...  17.1 us
    pallas_call x1, Pallas kernels, share(): pl.pallas_call(share_kernel, name='share', out_shape=(jax.ShapeDtypeStruc...  13.5 us
    unnamed x19, local copies, waits for them, and re-layouts  12.1 us
    ppermute x12, waiting for transfers between devices, moved(): return lax.ppermute(block, 'row', along(j, first))  11.4 us
    pallas_call x1, Pallas kernels, panel_roots(): pl.pallas_call(panel_roots_kernel, name='panel_roots', out_shape=(jax.Sha...  9.39 us
  transfers between devices with their start and end apart: 12, of which 1 were waited for; matrix products, arithmetic and copies ran while one was open for 4% of the time, Pallas kernels for 32%

profile of v2, /device:TPU:8, one launch (start us, length us, event | category | flops | bytes accessed | tf_op | source)
XLA Modules:
  0.0 209.9 jit_solution(8738291438463219986)
XLA Ops:
  0.6 8.3 %copy.13 = bf16[768,2,2048]{2,0,1:T(8,128)(2,1)} copy(bf16[768,2,2048]{2,1,0:T(2,128)(2,1)} %param.13) | data formatting | bytes 12582912 | tf_op args[6]
  9.0 17.1 %gather_all.1 = (f32[16,32,128]{2,1,0:T(8,128)}, f32[16,32,128]{2,1,0:T(8,128)}, f32[8,64,128]{2,1,0:T(8,128)}) custom-call(f32[32,128]{1,0:T(8,128)} %bitcast.57, f32[32,128]{1,0:T(8,128)} %bitcast.58, f32[64,128]{1,0:T(8,128)} %bitcast.55), custom_call_target="tpu_custom_call" | custom-call | tf_op jit(solution)/shard_map/gather_all/pallas_call | solution.py:90
  26.1 9.4 %panel_roots.1 = (f32[1,128]{1,0:T(1,128)}, f32[8,128]{1,0:T(8,128)}) custom-call(s32[2048]{0:T(1024)} %ch_ref.1, f32[512,128]{1,0:T(8,128)} %bitcast.61, f32[512,128]{1,0:T(8,128)} %bitcast.64, f32[512,128]{1,0:T(8,128)} %bitcast.67, s32[2,2048]{1,0:T(2,128)} %cp_ref.1), custom_call_target="tpu_custom_call" | custom-call | flops 30000000 | bytes 1048576 | tf_op jit(solution)/shard_map/panel_roots/pallas_call | solution.py:193
  35.5 13.5 %share.1 = (f32[16,8,1,128]{3,2,1,0:T(1,128)}, f32[8,8,128]{2,1,0:T(8,128)}) custom-call(f32[1,128]{1,0:T(1,128)} %get-tuple-element.38.tbl_ref, f32[8,128]{1,0:T(8,128)} %get-tuple-element.39.pw_ref), custom_call_target="tpu_custom_call" | custom-call | tf_op jit(solution)/shard_map/share/pallas_call | solution.py:227
  48.9 26.0 %product.1 = (f32[192,2048]{1,0:T(8,128)}, bf16[192,2048]{1,0:T(8,128)(2,1)}, bf16[192,2048]{1,0:T(8,128)(2,1)}, bf16[192,2048]{1,0:T(8,128)(2,1)}, f32[192,2048...) custom-call(f32[128,128]{1,0:T(8,128)} %bitcast.68, ...), custom_call_target="tpu_custom_call" | custom-call | flops 12999999488 | bytes 20971520 | tf_op jit(solution)/shard_map/product/pallas_call | solution.py:295
  75.5 3.0 %collective-permute-start.1 = (bf16[192,2048]{1,0:T(8,128)(2,1)}, bf16[192,2048]{1,0:T(8,128)(2,1)S(1)}, u32[]{:S(2)}, u32[]{:S(2)}) collective-permute-start(bf16[192,2048]{1,0:T(8,128)(2,1)} %get-tuple-element.44), channel_id=1, source_target_pairs={{0,64},{8,72},{16,80},{24,88},{32,96},{40,104},{48,112},{56,120},{... | collective-permute-start | bytes 2359304 | tf_op jit(solution)/shard_map/ppermute | solution.py:484
  80.4 2.8 %collective-permute-start.4 = (bf16[192,2048]{1,0:T(8,128)(2,1)}, bf16[192,2048]{1,0:T(8,128)(2,1)}, u32[]{:S(2)}, u32[]{:S(2)}) collective-permute-start(bf16[192,2048]{1,0:T(8,128)(2,1)} %get-tuple-element.48), channel_id=1, source_target_pairs={{0,16},{8,24},{16,0},{24,8},{32,48},{40,56},{48,32},{56,40},{64,80... | collective-permute-start | bytes 2359304 | tf_op jit(solution)/shard_map/ppermute | solution.py:484
  83.3 1.3 constant_dynamic-slice_fusion.1
  85.1 11.4 %collective-permute-done = bf16[192,2048]{1,0:T(8,128)(2,1)S(1)} collective-permute-done((bf16[192,2048]{1,0:T(8,128)(2,1)}, bf16[192,2048]{1,0:T(8,128)(2,1)S(1)}, u32[]{:S(2)}, u32[]{:S(2)}) %collective-permute-start) | collective-permute-done | bytes 786464 | tf_op jit(solution)/shard_map/ppermute | solution.py:484
  96.5 2.1 %collective-permute-start.5 = (bf16[192,2048]{1,0:T(8,128)(2,1)}, bf16[192,2048]{1,0:T(8,128)(2,1)}, u32[]{:S(2)}, u32[]{:S(2)}) collective-permute-start(bf16[192,2048]{1,0:T(8,128)(2,1)} %get-tuple-element.49), channel_id=1, source_target_pairs={{0,24},{8,0},{16,8},{24,16},{32,56},{40,32},{48,40},{56,48},{64,88... | collective-permute-start | bytes 2359304 | tf_op jit(solution)/shard_map/ppermute | solution.py:484
  98.7 48.7 %roots3.1 = f32[3,128]{1,0:T(4,128)} custom-call(f32[512,128]{1,0:T(8,128)} %bitcast.62, f32[512,128]{1,0:T(8,128)} %bitcast.65, f32[3,128]{1,0:T(4,128)} %bitcast.60, f32[3,128]{1,0:T(4,128)} %bitcast.59), custom_call_target="tpu_custom_call" | custom-call | flops 35999997952 | bytes 1048576 | tf_op jit(solution)/shard_map/roots3/pallas_call | solution.py:425
  147.4 1.3 slice.14.t_ref
  150.8 2.2 %convert_add_fusion = f32[192,2048]{1,0:T(8,128)S(1)} fusion(bf16[192,2048]{1,0:T(8,128)(2,1)} %collective-permute-done.5, bf16[192,2048]{1,0:T(8,128)(2,1)} %collective-permute-done.4, f32[192,2048]{1,0:T(8,128)S(1)} %copy-done.2, bf16[192,2048]{1,0:T(8,128)(2,1)} %collective-permute-done.3), kind=kLoop, calls=%fused_computation.1 | loop fusion | flops 2359296 | bytes 5505024 | tf_op jit(solution)/shard_map/add | solution.py:497
  153.8 14.1 %collective-permute-start.10 = (bf16[48,2048]{1,0:T(8,128)(2,1)S(1)}, bf16[48,2048]{1,0:T(8,128)(2,1)S(1)}, u32[]{:S(2)}, u32[]{:S(2)}) collective-permute-start(bf16[48,2048]{1,0:T(8,128)(2,1)S(1)} %get-tuple-element.71), channel_id=1, source_target_pairs={{0,64},{8,72},{16,80},{24,88},{32,96},{40,104},{48,112},{56,120},{... | collective-permute-start | bytes 589832 | tf_op jit(solution)/shard_map/ppermute | solution.py:484
  168.0 2.0 collective-permute-start.9
  170.0 1.6 convert_add_fusion.1
  172.4 1.8 collective-permute-start.6
  174.3 2.7 %collective-permute-start.8 = (bf16[48,2048]{1,0:T(8,128)(2,1)}, bf16[48,2048]{1,0:T(8,128)(2,1)}, u32[]{:S(2)}, u32[]{:S(2)}) collective-permute-start(bf16[48,2048]{1,0:T(8,128)(2,1)} %get-tuple-element.73), channel_id=1, source_target_pairs={{0,24},{8,0},{16,8},{24,16},{32,56},{40,32},{48,40},{56,48},{64,88... | collective-permute-start | bytes 589832 | tf_op jit(solution)/shard_map/ppermute | solution.py:484
  176.9 18.1 %roots1.1 = f32[1,128]{1,0:T(1,128)} custom-call(f32[512,128]{1,0:T(8,128)} %bitcast.63, f32[512,128]{1,0:T(8,128)} %bitcast.66, f32[1,128]{1,0:T(1,128)} %slice.15.c_ref, f32[1,128]{1,0:T(1,128)} %slice.14.t_ref), custom_call_target="tpu_custom_call" | custom-call | flops 12000000000 | bytes 1048576 | tf_op jit(solution)/shard_map/roots1/pallas_call | solution.py:425
  195.1 1.2 pad_maximum_fusion.1.t_ref
  196.4 1.5 fusion.2
  197.9 1.5 copy.11
  199.4 9.2 %finish.1 = f32[16,4,128]{2,1,0:T(4,128)} custom-call(f32[4,128]{1,0:T(4,128)} %pad_maximum_fusion.1.t_ref), custom_call_target="tpu_custom_call" | custom-call | tf_op jit(solution)/shard_map/finish/pallas_call | solution.py:454
  208.6 1.4 copy.15
  (37 shorter events, 6.8 us)
Async XLA Ops:
  0.6 83.9 %copy-start = (f32[8192]{0:T(1024)S(1)}, f32[8192]{0:T(1024)}, u32[]{:S(2)}) copy-start(f32[8192]{0:T(1024)} %param.9) | copy-start | bytes 98308
  75.0 21.5 %collective-permute-start = (bf16[192,2048]{1,0:T(8,128)(2,1)}, bf16[192,2048]{1,0:T(8,128)(2,1)S(1)}, u32[]{:S(2)}, u32[]{:S(2)}) collective-permute-start(bf16[192,2048]{1,0:T(8,128)(2,1)} %get-tuple-element.43), channel_id=1, source_target_pairs={{0,32},{8,40},{16,48},{24,56},{32,64},{40,72},{48,80},{56,88},{64,... | collective-permute-start | bytes 2359304 | tf_op jit(solution)/shard_map/ppermute | solution.py:484
  75.5 74.4 %collective-permute-start.1 = (bf16[192,2048]{1,0:T(8,128)(2,1)}, bf16[192,2048]{1,0:T(8,128)(2,1)S(1)}, u32[]{:S(2)}, u32[]{:S(2)}) collective-permute-start(bf16[192,2048]{1,0:T(8,128)(2,1)} %get-tuple-element.44), channel_id=1, source_target_pairs={{0,64},{8,72},{16,80},{24,88},{32,96},{40,104},{48,112},{56,120},{... | collective-permute-start | bytes 2359304 | tf_op jit(solution)/shard_map/ppermute | solution.py:484
  78.5 71.3 %collective-permute-start.2 = (bf16[192,2048]{1,0:T(8,128)(2,1)}, bf16[192,2048]{1,0:T(8,128)(2,1)}, u32[]{:S(2)}, u32[]{:S(2)}) collective-permute-start(bf16[192,2048]{1,0:T(8,128)(2,1)} %get-tuple-element.45), channel_id=1, source_target_pairs={{0,96},{8,104},{16,112},{24,120},{32,0},{40,8},{48,16},{56,24},{64... | collective-permute-start | bytes 2359304 | tf_op jit(solution)/shard_map/ppermute | solution.py:484
  79.7 70.2 %collective-permute-start.3 = (bf16[192,2048]{1,0:T(8,128)(2,1)}, bf16[192,2048]{1,0:T(8,128)(2,1)}, u32[]{:S(2)}, u32[]{:S(2)}) collective-permute-start(bf16[192,2048]{1,0:T(8,128)(2,1)} %get-tuple-element.47), channel_id=1, source_target_pairs={{0,8},{8,16},{16,24},{24,0},{32,40},{40,48},{48,56},{56,32},{64,72... | collective-permute-start | bytes 2359304 | tf_op jit(solution)/shard_map/ppermute | solution.py:484
  80.4 69.5 %collective-permute-start.4 = (bf16[192,2048]{1,0:T(8,128)(2,1)}, bf16[192,2048]{1,0:T(8,128)(2,1)}, u32[]{:S(2)}, u32[]{:S(2)}) collective-permute-start(bf16[192,2048]{1,0:T(8,128)(2,1)} %get-tuple-element.48), channel_id=1, source_target_pairs={{0,16},{8,24},{16,0},{24,8},{32,48},{40,56},{48,32},{56,40},{64,80... | collective-permute-start | bytes 2359304 | tf_op jit(solution)/shard_map/ppermute | solution.py:484
  96.5 50.9 %copy-start.3 = (bf16[192,2048]{1,0:T(8,128)(2,1)}, bf16[192,2048]{1,0:T(8,128)(2,1)S(1)}, u32[]{:S(2)}) copy-start(bf16[192,2048]{1,0:T(8,128)(2,1)S(1)} %collective-permute-done) | copy-start | bytes 2359300
  96.5 54.2 %collective-permute-start.5 = (bf16[192,2048]{1,0:T(8,128)(2,1)}, bf16[192,2048]{1,0:T(8,128)(2,1)}, u32[]{:S(2)}, u32[]{:S(2)}) collective-permute-start(bf16[192,2048]{1,0:T(8,128)(2,1)} %get-tuple-element.49), channel_id=1, source_target_pairs={{0,24},{8,0},{16,8},{24,16},{32,56},{40,32},{48,40},{56,48},{64,88... | collective-permute-start | bytes 2359304 | tf_op jit(solution)/shard_map/ppermute | solution.py:484
  98.7 52.1 %copy-start.2 = (f32[192,2048]{1,0:T(8,128)S(1)}, f32[192,2048]{1,0:T(8,128)}, u32[]{:S(2)}) copy-start(f32[192,2048]{1,0:T(8,128)} %get-tuple-element.55) | copy-start | bytes 4718596
  149.9 0.9 copy-start.5
  150.8 19.2 %copy-start.1 = (f32[192,2048]{1,0:T(8,128)S(1)}, f32[192,2048]{1,0:T(8,128)}, u32[]{:S(2)}) copy-start(f32[192,2048]{1,0:T(8,128)} %get-tuple-element.50) | copy-start | bytes 4718596
  150.8 19.2 %copy-start.6 = (bf16[192,2048]{1,0:T(8,128)(2,1)S(1)}, bf16[192,2048]{1,0:T(8,128)(2,1)}, u32[]{:S(2)}) copy-start(bf16[192,2048]{1,0:T(8,128)(2,1)} %copy-done.5) | copy-start | bytes 2359300
  153.0 17.0 %copy-start.4 = (bf16[192,2048]{1,0:T(8,128)(2,1)S(1)}, bf16[192,2048]{1,0:T(8,128)(2,1)}, u32[]{:S(2)}) copy-start(bf16[192,2048]{1,0:T(8,128)(2,1)} %copy-done.3) | copy-start | bytes 2359300
  153.8 20.4 %collective-permute-start.10 = (bf16[48,2048]{1,0:T(8,128)(2,1)S(1)}, bf16[48,2048]{1,0:T(8,128)(2,1)S(1)}, u32[]{:S(2)}, u32[]{:S(2)}) collective-permute-start(bf16[48,2048]{1,0:T(8,128)(2,1)S(1)} %get-tuple-element.71), channel_id=1, source_target_pairs={{0,64},{8,72},{16,80},{24,88},{32,96},{40,104},{48,112},{56,120},{... | collective-permute-start | bytes 589832 | tf_op jit(solution)/shard_map/ppermute | solution.py:484
  168.0 28.4 %collective-permute-start.11 = (bf16[48,2048]{1,0:T(8,128)(2,1)}, bf16[48,2048]{1,0:T(8,128)(2,1)}, u32[]{:S(2)}, u32[]{:S(2)}) collective-permute-start(bf16[48,2048]{1,0:T(8,128)(2,1)} %get-tuple-element.70), channel_id=1, source_target_pairs={{0,96},{8,104},{16,112},{24,120},{32,0},{40,8},{48,16},{56,24},{64... | collective-permute-start | bytes 589832 | tf_op jit(solution)/shard_map/ppermute | solution.py:484
  168.0 28.4 %collective-permute-start.9 = (bf16[48,2048]{1,0:T(8,128)(2,1)}, bf16[48,2048]{1,0:T(8,128)(2,1)}, u32[]{:S(2)}, u32[]{:S(2)}) collective-permute-start(bf16[48,2048]{1,0:T(8,128)(2,1)} %get-tuple-element.72), channel_id=1, source_target_pairs={{0,32},{8,40},{16,48},{24,56},{32,64},{40,72},{48,80},{56,88},{64,... | collective-permute-start | bytes 589832 | tf_op jit(solution)/shard_map/ppermute | solution.py:484
  172.4 23.9 %collective-permute-start.6 = (bf16[48,2048]{1,0:T(8,128)(2,1)}, bf16[48,2048]{1,0:T(8,128)(2,1)}, u32[]{:S(2)}, u32[]{:S(2)}) collective-permute-start(bf16[48,2048]{1,0:T(8,128)(2,1)} %get-tuple-element.75), channel_id=1, source_target_pairs={{0,8},{8,16},{16,24},{24,0},{32,40},{40,48},{48,56},{56,32},{64,72... | collective-permute-start | bytes 589832 | tf_op jit(solution)/shard_map/ppermute | solution.py:484
  174.3 22.1 %collective-permute-start.7 = (bf16[48,2048]{1,0:T(8,128)(2,1)}, bf16[48,2048]{1,0:T(8,128)(2,1)}, u32[]{:S(2)}, u32[]{:S(2)}) collective-permute-start(bf16[48,2048]{1,0:T(8,128)(2,1)} %get-tuple-element.74), channel_id=1, source_target_pairs={{0,16},{8,24},{16,0},{24,8},{32,48},{40,56},{48,32},{56,40},{64,80... | collective-permute-start | bytes 589832 | tf_op jit(solution)/shard_map/ppermute | solution.py:484
  174.3 20.8 %copy-start.7 = (f32[3,128]{1,0:T(4,128)S(1)}, f32[3,128]{1,0:T(4,128)}, u32[]{:S(2)}) copy-start(f32[3,128]{1,0:T(4,128)} %roots3.1) | copy-start | bytes 4612
  174.3 22.1 %collective-permute-start.8 = (bf16[48,2048]{1,0:T(8,128)(2,1)}, bf16[48,2048]{1,0:T(8,128)(2,1)}, u32[]{:S(2)}, u32[]{:S(2)}) collective-permute-start(bf16[48,2048]{1,0:T(8,128)(2,1)} %get-tuple-element.73), channel_id=1, source_target_pairs={{0,24},{8,0},{16,8},{24,16},{32,56},{40,32},{48,40},{56,48},{64,88... | collective-permute-start | bytes 589832 | tf_op jit(solution)/shard_map/ppermute | solution.py:484

commit v3 on v2

--- a/solution.py
+++ b/solution.py
@@ -1,5 +1,3 @@
-import functools
-
 import jax
 import jax.numpy as jnp
 from jax import lax
@@ -324,12 +322,12 @@
     return first, (exact + turn * step).astype(BF16)
 
 
-def root_block(b, first, p_ref, w_ref, c_ref, t_ref, out_ref, wa, wv, pd, pb, xs, a1, a2):
+def root_block(b, first, local, p_ref, w_ref, c_ref, t_ref, out_ref, wa, wv, pd, pb, xs, a1, a2):
     lane = lax.broadcasted_iota(jnp.int32, (1, 128), 1)
-    c = c_ref[pl.ds(b, 1), :]
+    c = c_ref[pl.ds(local + b, 1), :]
     own = p_ref[pl.ds(first + b, 1), :]
     origin = own[:, 64:65]
-    start = jnp.clip(lax.div(first + b, 2) - WINDOW // 2, 0, PAIRS - WINDOW)
+    near_rows = [lax.rem(lax.div(first + b, 2) + PAIRS - WINDOW // 2 + k, PAIRS) for k in range(WINDOW)]
     pd[...] = p_ref[...] - origin
 
     def fill(q, _):
@@ -338,10 +336,10 @@
         return 0
 
     lax.fori_loop(0, PAIRS, fill, 0, unroll=8)
-    for k in range(WINDOW):
-        wa[start + k] = jnp.zeros((8, 256), BF16)
-        wv[start + k] = jnp.zeros((8, 256), BF16)
-        pb[start + k] = jnp.full((8, 256), 8192.0, BF16)
+    for q in near_rows:
+        wa[q] = jnp.zeros((8, 256), BF16)
+        wv[q] = jnp.zeros((8, 256), BF16)
+        pb[q] = jnp.full((8, 256), 8192.0, BF16)
     one = jnp.ones((8, 256), BF16)
     h = c - own
     last = (first + b) * 128 + lane == N - 1
@@ -375,8 +373,9 @@
             far = lax.fori_loop(0, PAIRS // CHAIN, chain, ((zero, zero), (zero, zero)))
             near = [[f[:, :128] + f[:, 128:] for f in fs] for fs in far]
             for i in range(2 * WINDOW):
-                pole = pd[pl.ds(2 * start + i, 1), :]
-                w = w_ref[pl.ds(2 * start + i, 1), :]
+                at = pl.ds(2 * near_rows[i // 2] + i % 2, 1)
+                pole = pd[at, :]
+                w = w_ref[at, :]
                 wsq = w * w
                 for k in range(2):
                     inverse = 1.0 / (pole - x_g[k])
@@ -395,120 +394,143 @@
         nearest = jnp.where(last, left, jnp.minimum(left, right))
         return limited(t, s1, s2, nearest)
 
-    out_ref[pl.ds(b, 1), :] = lax.fori_loop(0, ITERS, iteration, t_ref[pl.ds(b, 1), :])
-    for k in range(WINDOW):
-        wa[start + k], wv[start + k] = weight_tables(w_ref, start + k)
-
-
-def roots_kernel(p_ref, w_ref, c_ref, t_ref, out_ref, wa, wv, *scratch):
+    out_ref[pl.ds(b, 1), :] = lax.fori_loop(0, ITERS, iteration, t_ref[pl.ds(local + b, 1), :])
+    for q in near_rows:
+        wa[q], wv[q] = weight_tables(w_ref, q)
+
+
+SPLIT = 3
+WIDE = 256
+
+
+def tail_kernel(
+    p_ref, w_ref, c_ref, t_ref, own_z, own_x, z1, z2, z3, x1, x2, x3, t_out, panel_out,
+    mine, got, out2, got2, t_new, wa, wv, pd, pb, xs, a1, a2,
+    s1, r1, s2, r2, s3, r3, ls,
+):
     row, col = lax.axis_index("row"), lax.axis_index("col")
-    first = col * 64 + row * 4 + (4 - t_ref.shape[0]) * FIRST_OF[t_ref.shape[0]]
+    z, x = lax.div(row, 4), lax.rem(row, 4)
+    barrier = pltpu.get_barrier_semaphore()
+    for j in range(1, ROWS):
+        pl.semaphore_signal(barrier, inc=1, device_id={"row": lax.rem(row + j, ROWS)}, device_id_type=MESH)
+    local = [pltpu.make_async_copy(own_z, mine.at[0], ls.at[0]), pltpu.make_async_copy(own_x, mine.at[1], ls.at[1])]
+    for c in local:
+        c.start()
+    pl.semaphore_wait(barrier, ROWS - 1)
+
+    def peer(j, along_z):
+        return lax.rem(z + j, 4) * 4 + x if along_z else z * 4 + lax.rem(x + j, 4)
+
+    def exchange(sources, target, send, recv, swap):
+        copies = []
+        for i, source in enumerate(sources):
+            copies.append(
+                pltpu.make_async_remote_copy(
+                    src_ref=source,
+                    dst_ref=target.at[i],
+                    send_sem=send.at[i],
+                    recv_sem=recv.at[i],
+                    device_id={"row": peer(i % 3 + 1, (i < 3) != swap)},
+                    device_id_type=MESH,
+                )
+            )
+        for i in (1, 4, 0, 3, 2, 5):
+            copies[i].start()
+        return copies
+
+    first_copies = exchange((z1, z2, z3, x1, x2, x3), got, s1, r1, False)
 
     def fill(q, _):
         wa[q], wv[q] = weight_tables(w_ref, q)
         return 0
 
     lax.fori_loop(0, PAIRS, fill, 0, unroll=4)
+    first = col * 64 + row * 4
 
     def block(b, _):
-        root_block(b, first, p_ref, w_ref, c_ref, t_ref, out_ref, wa, wv, *scratch)
+        root_block(b, first, row * 4, p_ref, w_ref, c_ref, t_ref, t_new, wa, wv, pd, pb, xs, a1, a2)
         return 0
 
-    lax.fori_loop(0, t_ref.shape[0], block, 0)
-
-
-FIRST_OF = {3: 0, 1: 1}
-
-
-def roots(poles, weights, centers, offsets):
-    blocks = offsets.shape[0]
+    lax.fori_loop(0, SPLIT, block, 0)
+    for c in local:
+        c.wait()
+    for c in first_copies:
+        c.wait()
+
+    def add(i, _):
+        lanes = pl.ds(pl.multiple_of(i * WIDE, WIDE), WIDE)
+        for half in range(2):
+            me = x if half == 0 else z
+            for j in range(4):
+                at = pl.ds(pl.multiple_of(lax.rem(me + j, 4) * 48, 48), 48)
+                total = mine[half, at, lanes]
+                for k in range(3):
+                    total = total + got[half * 3 + k, at, lanes].astype(F32)
+                if j:
+                    out2[half * 3 + j - 1, :, lanes] = total
+                else:
+                    panel_out[half, :, lanes] = total
+        return 0
+
+    lax.fori_loop(0, PANEL // WIDE, add, 0)
+    second_copies = exchange([out2.at[i] for i in range(6)], got2, s2, r2, True)
+    lax.fori_loop(SPLIT, 4, block, 0)
+    own = pltpu.make_async_copy(t_new, t_out.at[row], ls.at[2])
+    own.start()
+    third = spread(t_new, t_out, "row", ROWS, row, s3, r3)
+    for c in second_copies:
+        c.wait()
+
+    def last_add(i, _):
+        lanes = pl.ds(pl.multiple_of(i * WIDE, WIDE), WIDE)
+        for half in range(2):
+            total = panel_out[half, :, lanes]
+            for k in range(3):
+                total = total + got2[half * 3 + k, :, lanes]
+            panel_out[half, :, lanes] = total
+        return 0
+
+    lax.fori_loop(0, PANEL // WIDE, last_add, 0)
+    collect(third, t_new, t_out, "row", ROWS, row, s3, r3)
+    own.wait()
+
+
+def tail(poles, weights, centers, offsets, blocks):
+    anywhere = pl.BlockSpec(memory_space=pl.ANY)
     return pl.pallas_call(
-        roots_kernel,
-        name=f"roots{blocks}",
-        out_shape=jax.ShapeDtypeStruct((blocks, 128), F32),
-        in_specs=[vmem()] * 4,
-        out_specs=vmem(),
-        scratch_shapes=[VMEM((PAIRS, 8, 256), BF16)] * 2
-        + [VMEM((TILES, 128), F32), VMEM((PAIRS, 8, 256), BF16)]
-        + [VMEM((128, 128), F32)] * 3,
-        cost_estimate=pl.CostEstimate(
-            flops=blocks * 12_000_000_000, bytes_accessed=1 << 20, transcendentals=33_000_000
-        ),
-    )(poles, weights, centers, offsets)
-
-
-def finish_kernel(t_ref, out_ref, ts, tr, ls):
-    row = lax.axis_index("row")
-    own = pltpu.make_async_copy(t_ref, out_ref.at[row], ls.at[0])
-    own.start()
-    barrier = pltpu.get_barrier_semaphore()
-    for j in range(1, ROWS):
-        pl.semaphore_signal(barrier, inc=1, device_id={"row": lax.rem(row + j, ROWS)}, device_id_type=MESH)
-    pl.semaphore_wait(barrier, ROWS - 1)
-    a = spread(t_ref, out_ref, "row", ROWS, row, ts, tr)
-    collect(a, t_ref, out_ref, "row", ROWS, row, ts, tr)
-    own.wait()
-
-
-def finish(t):
-    return pl.pallas_call(
-        finish_kernel,
-        name="finish",
-        out_shape=jax.ShapeDtypeStruct((ROWS, 4, 128), F32),
-        in_specs=[vmem()],
-        out_specs=vmem(),
-        scratch_shapes=[dma(15), dma(15), dma(1)],
+        tail_kernel,
+        name="tail",
+        out_shape=(jax.ShapeDtypeStruct((ROWS, 4, 128), F32), jax.ShapeDtypeStruct((2, 48, PANEL), F32)),
+        in_specs=[vmem()] * 4 + [anywhere] * 8,
+        out_specs=(vmem(), vmem()),
+        scratch_shapes=[
+            VMEM((2, 192, PANEL), F32),
+            VMEM((6, 192, PANEL), BF16),
+            VMEM((6, 48, PANEL), F32),
+            VMEM((6, 48, PANEL), F32),
+            VMEM((4, 128), F32),
+            VMEM((PAIRS, 8, 256), BF16),
+            VMEM((PAIRS, 8, 256), BF16),
+            VMEM((TILES, 128), F32),
+            VMEM((PAIRS, 8, 256), BF16),
+            VMEM((128, 128), F32),
+            VMEM((128, 128), F32),
+            VMEM((128, 128), F32),
+            dma(6), dma(6), dma(6), dma(6), dma(15), dma(15), dma(3),
+        ],
         compiler_params=pltpu.CompilerParams(collective_id=2, has_side_effects=True),
-    )(t)
-
-
-def along(j, first):
-    pairs = []
-    for z in range(4):
-        for x in range(4):
-            to = ((z + j) % 4, x) if first else (z, (x + j) % 4)
-            pairs.append((z * 4 + x, to[0] * 4 + to[1]))
-    return pairs
+    )(poles, weights, centers, offsets, *blocks)
 
 
 def on_device(pole_values, weights, centers, offsets, chosen, column_pole, eigen_blocks):
-    row = lax.axis_index("row")
-    z, x = lax.div(row, 4), lax.rem(row, 4)
     all_p, all_w, all_o = gather_all(pole_values, weights, offsets)
     all_p, all_w, all_o = (a.reshape(TILES, 128) for a in (all_p, all_w, all_o))
     tbl, pw = share(*panel_roots(chosen, all_p, all_w, all_o, column_pole))
     halves = jnp.transpose(eigen_blocks, (1, 0, 2))
     blocks = product(tbl.reshape(128, 128), pw, halves)
-
-    def moved(block, j, first):
-        return lax.ppermute(block, "row", along(j, first))
-
-    got = [[moved(blocks[4 * half + j], j, half == 0) for j in (1, 2, 3)] for half in range(2)]
-
-    my_centers = lax.dynamic_slice_in_dim(centers.reshape(64, 128), row * 4, 4)
-    t = lax.dynamic_slice_in_dim(offsets.reshape(64, 128), row * 4, 4)
-    t, blocks = lax.optimization_barrier((t, blocks))
-    t_most = roots(all_p, all_w, my_centers[:3], t[:3])
-    got, t_most, t_rest = lax.optimization_barrier((got, t_most, t[3:]))
-    panels, sent = [], []
-    for half in range(2):
-        total = blocks[4 * half]
-        for g in got[half]:
-            total = total + g.astype(F32)
-        total = total.reshape(4, 48, PANEL)
-        me = x if half == 0 else z
-        sent.append([
-            moved(lax.dynamic_index_in_dim(total, lax.rem(me + j, 4), 0, False).astype(BF16), j, half == 1)
-            for j in (1, 2, 3)
-        ])
-        panels.append(lax.dynamic_index_in_dim(total, me, 0, False))
-    t = jnp.concatenate([t_most, roots(all_p, all_w, my_centers[3:], t_rest)])
-    sent, t = lax.optimization_barrier((sent, t))
-    offset_now = finish(t).reshape(8192)
-    for half in range(2):
-        for g in sent[half]:
-            panels[half] = panels[half] + g.astype(F32)
-    return offset_now, jnp.stack(panels, axis=1)
+    blocks = (blocks[0], blocks[4], *blocks[1:4], *blocks[5:8])
+    t, panel = tail(all_p, all_w, centers.reshape(64, 128), offsets.reshape(64, 128), blocks)
+    return t.reshape(8192), jnp.transpose(panel, (1, 0, 2))
 
 
 def solution(mesh):

time: 211 us -> 155 us (0.73)
  starting transfers between devices: 31.1 us -> 0 us
  waiting for transfers between devices: 11.4 us -> 0 us
  other arithmetic: 6.56 us -> 0 us
  local copies, waits for them, and re-layouts: 18.1 us -> 12.3 us
  Pallas kernels: 142 us -> 139 us
    ppermute x12 -> x0, starting transfers between devices: 31.1 us -> none  [moved(): return lax.ppermute(block, 'row', along(j, first))]
    ppermute x12 -> x0, waiting for transfers between devices: 11.4 us -> none  [moved(): return lax.ppermute(block, 'row', along(j, first))]
    add x2 -> x0, other arithmetic: 3.8 us -> none  [on_device(): total = total + g.astype(F32)]
    pallas_call x3 -> x1, Pallas kernels: 76 us -> 73.4 us  [tail(): pl.pallas_call(tail_kernel, name='tail', out_shape=(jax.ShapeDtypeStruct(...]
    slice x2 -> x0, local copies, waits for them, and re-layouts: 2.47 us -> none  [the longest x1 1.27 us: on_device(): got, t_most, t_rest = lax.optimization_barrier((got, t_most, t[3:]))]
    unnamed x19 -> x3, local copies, waits for them, and re-layouts: 12.1 us -> 12.3 us
  transfers between devices with their start and end apart: 12 -> 0, of which waited for: 1 -> 0; matrix products, arithmetic and copies ran while one was open for 4% -> 0% of each run, Pallas kernels for 32% -> 0%
where the time goes in v3:
time: 155 us; the launch traced here: 152 us
  Pallas kernels  139 us (90%)
  local copies, waits for them, and re-layouts  12.3 us (8%)
    pallas_call x1, Pallas kernels, tail(): pl.pallas_call(tail_kernel, name='tail', out_shape=(jax.ShapeDtypeStruct(...  73.4 us
    pallas_call x1, Pallas kernels, product(): pl.pallas_call(product_kernel, name='product', grid=(2, steps), out_shape...  26 us
    pallas_call x1, Pallas kernels, gather_all(): pl.pallas_call(gather_kernel, name='gather_all', out_shape=(jax.ShapeDtyp...  17.2 us
    pallas_call x1, Pallas kernels, share(): pl.pallas_call(share_kernel, name='share', out_shape=(jax.ShapeDtypeStruc...  13.5 us
    unnamed x3, local copies, waits for them, and re-layouts  12.3 us
    pallas_call x1, Pallas kernels, panel_roots(): pl.pallas_call(panel_roots_kernel, name='panel_roots', out_shape=(jax.Sha...  9.39 us

profile of v3, /device:TPU:8, one launch (start us, length us, event | category | flops | bytes accessed | tf_op | source)
XLA Modules:
  0.0 152.4 jit_solution(10642957506424831091)
XLA Ops:
  0.6 17.2 %gather_all.1 = (f32[16,32,128]{2,1,0:T(8,128)}, f32[16,32,128]{2,1,0:T(8,128)}, f32[8,64,128]{2,1,0:T(8,128)}) custom-call(f32[32,128]{1,0:T(8,128)} %bitcast.23, f32[32,128]{1,0:T(8,128)} %bitcast.24, f32[64,128]{1,0:T(8,128)} %bitcast.19), custom_call_target="tpu_custom_call" | custom-call | tf_op jit(solution)/shard_map/gather_all/pallas_call | solution.py:88
  17.8 9.4 %panel_roots.1 = (f32[1,128]{1,0:T(1,128)}, f32[8,128]{1,0:T(8,128)}) custom-call(s32[2048]{0:T(1024)} %ch_ref.1, f32[512,128]{1,0:T(8,128)} %bitcast.15, f32[512,128]{1,0:T(8,128)} %bitcast.17, f32[512,128]{1,0:T(8,128)} %bitcast.25, s32[2,2048]{1,0:T(2,128)} %cp_ref.1), custom_call_target="tpu_custom_call" | custom-call | flops 30000000 | bytes 1048576 | tf_op jit(solution)/shard_map/panel_roots/pallas_call | solution.py:191
  27.2 13.5 %share.1 = (f32[16,8,1,128]{3,2,1,0:T(1,128)}, f32[8,8,128]{2,1,0:T(8,128)}) custom-call(f32[1,128]{1,0:T(1,128)} %get-tuple-element.22.tbl_ref, f32[8,128]{1,0:T(8,128)} %get-tuple-element.23.pw_ref), custom_call_target="tpu_custom_call" | custom-call | tf_op jit(solution)/shard_map/share/pallas_call | solution.py:225
  40.7 8.3 %copy.12 = bf16[768,2,2048]{2,0,1:T(8,128)(2,1)} copy(bf16[768,2,2048]{2,1,0:T(2,128)(2,1)} %param.13) | data formatting | bytes 12582912 | tf_op args[6]
  49.0 26.0 %product.1 = (f32[192,2048]{1,0:T(8,128)}, bf16[192,2048]{1,0:T(8,128)(2,1)}, bf16[192,2048]{1,0:T(8,128)(2,1)}, bf16[192,2048]{1,0:T(8,128)(2,1)}, f32[192,2048...) custom-call(f32[128,128]{1,0:T(8,128)} %bitcast.26, ...), custom_call_target="tpu_custom_call" | custom-call | flops 12999999488 | bytes 20971520 | tf_op jit(solution)/shard_map/product/pallas_call | solution.py:293
  75.0 73.4 %tail.1 = (f32[16,4,128]{2,1,0:T(4,128)}, f32[2,48,2048]{2,1,0:T(8,128)}) custom-call(f32[512,128]{1,0:T(8,128)} %bitcast.16, f32[512,128]{1,0:T(8,128)} %bitcast.18, f32[64,128]{1,0:T(8,128)} %bitcast.21, f32[64,128]{1,0:T(8,128)} %bitcast.20, f32[192,2048]{1,0:T(8,128)} %get-tuple-element.26.own_z, f32[192,2048]{1,0:T(8,128)} %get-tuple-element.27.own_x, ...), custom_call_target="tpu_custom_call" | custom-call | tf_op jit(solution)/shard_map/tail/pallas_call | solution.py:500
  148.4 2.6 %copy.10 = f32[48,2,2048]{2,1,0:T(2,128)} copy(f32[48,2,2048]{2,0,1:T(8,128)} %bitcast.14) | data formatting | bytes 1572864
  151.0 1.4 copy.14
